TPU v7x, 256 devices: a whole 4x4x8 slice. The times are simulated.
256 devices in a mesh: seq: 16 (over z, x_lo), img: 8 (over y, x_hi), fsdp: 2 (over core).
Axes of the slice: x: 4 (x_hi: 2, x_lo: 2; x = x_hi * 2 + x_lo), y: 4, z: 8, core: 2. Of those that a mesh axis runs over, the one named last changes fastest.
Arguments:
- vision_feats: bfloat16 [8, 2304, 1024], P('img', ('seq', 'fsdp')), may hold values from -6 to 6
- ln_gain: float32 [1024], replicated, may hold values from 0.5 to 1.5
- ln_bias: float32 [1024], replicated, may hold values from -3 to 3
- w_in: bfloat16 [1024, 4096], P('fsdp', 'seq'), may hold values from -0.1875 to 0.1875
- b_in: float32 [4096], P('seq'), may hold values from -3 to 3
- w_out: bfloat16 [4096, 4096], P('seq', 'fsdp'), may hold values from -0.09375 to 0.09375
- lm_grad: bfloat16 [8, 4096, 4096], P('img', 'seq', 'fsdp'), may hold values from -0.079589844 to 0.079589844
- image_counts: int32 [8, 2], P('img'), may hold values from 1 to 3, as said below
- token_pos: int32 [8, 2304], P('img'), may hold values from 0 to 2047, as said below
Outputs:
- w_in_grad: float32 [1024, 4096], P(('img', 'fsdp'), 'seq')
- b_in_grad: float32 [4096], replicated
- w_out_grad: float32 [4096, 4096], P(('seq', 'img'), 'fsdp')
- b_out_grad: float32 [4096], replicated
- ln_gain_grad: float32 [1024], replicated
- ln_bias_grad: float32 [1024], replicated
Inputs may be any that keep to these rules, and one draw needn't show every extreme that they name: `image_counts`: in each group the 2 samples hold 4 images together, each sample one or more. `token_pos`: each image's 576 tokens take consecutive positions of its sample's sequence in order; a sample's images come in order without intersection, and images are numbered sample by sample as image_counts gives.
All inputs are finite; a program needn't handle non-finite values.
Results may differ from a plain program's by a relative error of at most 0.0047.
Values may be sent and summed in bfloat16 or wider, within the bound.
A program may use at most 128 MiB of HBM per device.

v0:
```python
import jax
import jax.numpy as jnp
from jax import lax
from jax.sharding import Mesh
from jax.sharding import PartitionSpec as P

PATCH = 576
LEN = 2048
SEQ = ("seq_0", "seq_1")
IMG = ("img_0", "img_1")
SEQ_FSDP = ("seq_0", "seq_1", "fsdp")
SEQ_IMG_FSDP = ("seq_0", "seq_1", "img_0", "img_1", "fsdp")
IMG_FSDP = ("img_0", "img_1", "fsdp")
SEQ_IMG = ("seq_0", "seq_1", "img_0", "img_1")


def copy_for_each(array, axis):
    copies = jnp.broadcast_to(array, (lax.axis_size(axis), *array.shape))
    return lax.all_to_all(copies, axis, split_axis=0, concat_axis=0, tiled=True)


def in_order(pieces, dim):
    shape = list(pieces.shape[1:])
    shape[dim] *= pieces.shape[0]
    return jnp.moveaxis(pieces, 0, dim).reshape(shape)


def gather_directly(array, axis, dim):
    pieces = copy_for_each(array, axis)
    return in_order(pieces, dim)


def whole_of(array, axes, dim):
    if not axes:
        return array
    nearer = lax.all_gather(array, axes[-1], axis=dim, tiled=True)
    return whole_of(nearer, axes[:-1], dim)


def taken_together(array, axis):
    return copy_for_each(array, axis).sum(axis=0)


def in_blocks(array, dim, devices):
    shape = array.shape
    pieces = array.reshape(*shape[:dim], devices, shape[dim] // devices, *shape[dim + 1 :])
    return jnp.moveaxis(pieces, dim, 0)


def one_scatter(arrays, axis, dims):
    devices = lax.axis_size(axis)
    pieces = [in_blocks(a, dim, devices) for a, dim in zip(arrays, dims)]
    lines = jnp.concatenate([b.reshape(devices, -1) for b in pieces], axis=1)
    width = max(16, -(-lines.shape[1] // 1024) * 8)
    lines = jnp.pad(lines, ((0, 0), (0, width * 128 - lines.shape[1]))).reshape(-1, 128)
    vector, at, gathered = (lax.psum_scatter(lines, axis, tiled=True).reshape(-1), 0, [])
    for b in pieces:
        part = b[0]
        gathered.append(vector[at : at + part.size].reshape(part.shape))
        at += part.size
    return tuple(gathered)


def one_axis_at_a_time(array, axes):
    for axis in axes:
        array = lax.psum(array, axis)
    return array


def gelu_parts(preact):
    cumul = 0.5 * (1.0 + lax.erf(preact * 0.7071067811865476))
    density = jnp.exp(-0.5 * preact * preact) * 0.3989422804014327
    return (preact * cumul, cumul + preact * density)


def contract(left, right, left_dim, right_dim):
    return lax.dot_general(
        left, right, (((left_dim,), (right_dim,)), ((), ())), preferred_element_type=jnp.float32
    )


def own_columns(matrix, img_count, fsdp_count, fsdp_index):
    rows = matrix.shape[0]
    block = matrix.shape[1] // (img_count * fsdp_count)
    shaped = matrix.reshape(rows, img_count, fsdp_count, block)
    taken = lax.dynamic_index_in_dim(shaped, fsdp_index, axis=2, keepdims=False)
    return taken.reshape(rows, img_count * block)


def place_columns(vector, img_count, fsdp_count, fsdp_index):
    block = vector.shape[0] // img_count
    holder = jnp.zeros((img_count, fsdp_count, block), jnp.float32)
    holder = lax.dynamic_update_slice(
        holder, vector.reshape(img_count, 1, block), (0, fsdp_index, 0)
    )
    return holder.reshape(img_count * fsdp_count * block)


def per_device(vision_feats, ln_gain, ln_bias, w_in, b_in, w_out, lm_grad, image_counts, token_pos):
    seq_count = lax.axis_size(SEQ)
    seq_index = lax.axis_index(SEQ)
    img_count = lax.axis_size(IMG)
    fsdp_count = lax.axis_size("fsdp")
    fsdp_index = lax.axis_index("fsdp")
    lm_block = lm_grad[0]
    block_rows = lm_block.shape[0]
    half_width = lm_block.shape[1]
    position_count = block_rows * seq_count
    counts = image_counts[0]
    positions = token_pos[0]
    row_count = positions.shape[0]
    image_index = jnp.arange(row_count, dtype=jnp.int32) // PATCH
    bounds = jnp.cumsum(counts)
    sample = jnp.sum((image_index[:, None] >= bounds[None, :]).astype(jnp.int32), axis=1)
    abs_pos = sample * LEN + positions
    marker = jnp.zeros((position_count,), jnp.float32).at[abs_pos].set(1.0)
    own_mask = lax.dynamic_slice_in_dim(marker, seq_index * block_rows, block_rows).astype(
        jnp.bfloat16
    )
    out_bias_half = jnp.dot(own_mask[None, :], lm_block, preferred_element_type=jnp.float32)[0]
    out_bias_full = lax.dynamic_update_slice_in_dim(
        jnp.zeros((half_width * fsdp_count,), jnp.float32),
        out_bias_half,
        fsdp_index * half_width,
        0,
    )
    w_in_full = gather_directly(w_in, "fsdp", 0)
    gathered = lax.all_gather(vision_feats[0], SEQ_FSDP, axis=0, tiled=True)
    values = gathered.astype(jnp.float32)
    row_mean = jnp.mean(values, axis=1, keepdims=True)
    centred = values - row_mean
    row_var = jnp.mean(centred * centred, axis=1, keepdims=True)
    normed = centred * lax.rsqrt(row_var + 1e-05)
    normed_in = (normed * ln_gain + ln_bias).astype(jnp.bfloat16)
    preact = jnp.dot(normed_in, w_in_full, preferred_element_type=jnp.float32) + b_in
    activ, slope = gelu_parts(preact)
    hidden = activ.astype(jnp.bfloat16)
    hidden_width = hidden.shape[1]
    whole_grad = whole_of(lm_block, SEQ, 0)
    picked = whole_grad[abs_pos]
    hidden_part = contract(picked, w_out, 1, 1)
    w_out_part = contract(hidden, picked, 0, 0)
    hidden_grad = taken_together(hidden_part, "fsdp")
    preact_grad = (hidden_grad * slope).astype(jnp.bfloat16)
    own_normed_in = own_columns(normed_in, img_count, fsdp_count, fsdp_index)
    own_normed = own_columns(normed, img_count, fsdp_count, fsdp_index)
    own_w_in = own_columns(w_in_full.T, img_count, fsdp_count, fsdp_index)
    w_in_part = contract(own_normed_in, preact_grad, 0, 0)
    half_rows = row_count // fsdp_count
    own_rows = lax.dynamic_slice_in_dim(preact_grad, fsdp_index * half_rows, half_rows, 0)
    b_in_part = jnp.sum(own_rows, axis=0, dtype=jnp.float32)
    normed_grad = contract(preact_grad, own_w_in, 1, 0)
    gain_part = place_columns(
        jnp.sum(normed_grad * own_normed, axis=0), img_count, fsdp_count, fsdp_index
    )
    bias_part = place_columns(jnp.sum(normed_grad, axis=0), img_count, fsdp_count, fsdp_index)
    w_in_grad, w_out_grad = one_scatter((w_in_part, w_out_part), IMG, (0, 0))
    hidden_full = lax.dynamic_update_slice_in_dim(
        jnp.zeros((hidden_width * seq_count,), jnp.float32), b_in_part, seq_index * hidden_width, 0
    )
    gain_grad, bias_grad, b_in_grad, b_out_grad = (
        one_axis_at_a_time(gain_part, SEQ_IMG_FSDP),
        one_axis_at_a_time(bias_part, SEQ_IMG_FSDP),
        one_axis_at_a_time(hidden_full, SEQ_IMG_FSDP),
        one_axis_at_a_time(out_bias_full, SEQ_IMG_FSDP),
    )
    return (w_in_grad, b_in_grad, w_out_grad, b_out_grad, gain_grad, bias_grad)


def solution(mesh):
    finer = Mesh(
        mesh.devices.reshape(8, 2, 4, 2, mesh.shape["fsdp"]),
        ("seq_0", "seq_1", "img_0", "img_1", "fsdp"),
    )
    placed = (
        P(IMG, SEQ_FSDP, None),
        P(),
        P(),
        P("fsdp", SEQ),
        P(SEQ),
        P(SEQ, "fsdp"),
        P(IMG, SEQ, "fsdp"),
        P(IMG, None),
        P(IMG, None),
    )
    return jax.shard_map(
        per_device,
        mesh=finer,
        in_specs=placed,
        out_specs=(P(IMG_FSDP, SEQ), P(), P(SEQ_IMG, "fsdp"), P(), P(), P()),
        check_vma=False,
    )
```

profile of v0, /device:TPU:1, one launch (start us, length us, event | category | flops | bytes accessed | tf_op | source)
XLA Modules:
  0.0 471.8 jit_solution(9273449355537463096)
XLA Ops:
  8.7 42.9 %all-gather.9.cloned.1.call-done = bf16[1,512,2048]{2,1,0:T(8,128)(2,1)} async-done(((bf16[1,256,2048]{2,1,0:T(8,128)(2,1)}), bf16[1,512,2048]{2,1,0:T(8,128)(2,1)}) %all-gather.9.cloned.1.call-update) | async-done | bytes 2097168 | tf_op jit(solution)/shard_map/all_gather | solution.py:36
  52.0 70.0 %all-gather.7.cloned.1.call-done = bf16[1,2304,1024]{2,1,0:T(8,128)(2,1)} async-done(((bf16[1,72,1024]{2,1,0:T(8,128)(2,1)}), bf16[1,2304,1024]{2,1,0:T(8,128)(2,1)}) %all-gather.7.cloned.1.call-update) | async-done | bytes 4718608 | tf_op jit(solution)/shard_map/all_gather | solution.py:128
  122.1 6.8 %copy.20 = bf16[1,2304,1024]{1,2,0:T(8,128)(2,1)} copy(bf16[1,2304,1024]{2,1,0:T(8,128)(2,1)} %all-gather.7.cloned.1.call-done) | data formatting | bytes 9437184 | tf_op jit(solution)/shard_map/all_gather | solution.py:128
  128.9 3.2 convert_reduce_fusion
  133.9 4.8 %fusion.1 = (f32[2304,1024]{0,1:T(8,128)}, bf16[2304,1024]{0,1:T(8,128)(2,1)S(1)}) fusion(bf16[1,2304,1024]{1,2,0:T(8,128)(2,1)S(1)} %copy-done.2, f32[2304]{0:T(1024)S(1)} %add_rsqrt_fusion, f32[2304]{0:T(1024)S(1)} %broadcast_multiply_fusion.1, f32[1024]{0:T(1024)S(1)} %copy-done.10, f32[1024]{0:T(1024)S(1)} %copy-done.11), kind=kLoop, calls=%fused_computation.5 | loop fusion | flops 14155776 | bytes 18900992 | tf_op jit(solution)/shard_map/mul | solution.py:133
  142.5 153.5 %all-gather.11.cloned.1.call-done = bf16[1,4096,2048]{2,1,0:T(8,128)(2,1)} async-done(((bf16[1,512,2048]{2,1,0:T(8,128)(2,1)}), bf16[1,4096,2048]{2,1,0:T(8,128)(2,1)}) %all-gather.11.cloned.1.call-update) | async-done | bytes 16777232 | tf_op jit(solution)/shard_map/all_gather | solution.py:36
  296.0 26.2 %gather_fusion = bf16[2304,2048]{1,0:T(8,128)(2,1)} fusion(bf16[4096,2048]{1,0:T(8,128)(2,1)} %bitcast.43, s32[3072]{0:T(1024)S(1)} %pad_clamp_fusion), kind=kCustom, calls=%fused_computation | custom fusion | bytes 18883584 | tf_op jit(solution)/shard_map/gather | solution.py:140
  322.2 5.2 %fusion.21 = f32[2304,256]{1,0:T(8,128)S(1)} fusion(bf16[2304,2048]{1,0:T(8,128)(2,1)} %gather_fusion, bf16[256,2048]{1,0:T(8,128)(2,1)S(1)} %copy-done), kind=kOutput, calls=%fused_computation.48 | convolution fusion | flops 2415919104 | bytes 12845056 | tf_op jit(solution)/shard_map/dot_general | solution.py:77
  327.8 9.2 %all_to_all.10 = f32[2,2304,256]{2,1,0:T(8,128)} all-to-all(f32[2,2304,256]{2,1,0:T(8,128)S(1)} %broadcast_in_dim.6), channel_id=1, replica_groups=mesh['seq_0'=8,'seq_1'=2,'img_0'=4,'img_1'=2,'fsdp'=2] {'fsdp'}, dimensions={0} | all-to-all | bytes 9437184 | tf_op jit(solution)/shard_map/all_to_all | solution.py:19
  337.9 3.8 all-to-all-start.1
  341.7 4.5 reduce_sum.66
  346.2 6.7 %fusion.9 = (bf16[2304,256]{1,0:T(8,128)(2,1)}, f32[2304,256]{1,0:T(8,128)S(1)}) fusion(f32[2304,256]{1,0:T(8,128)} %reduce_sum.66, f32[256]{0:T(256)S(1)} %copy-done.12, bf16[2304,1024]{0,1:T(8,128)(2,1)} %copy-done.3, bf16[1024,256]{1,0:T(8,128)(2,1)S(1)} %bitcast.50), kind=kOutput, calls=%fused_computation.18 | convolution fusion | flops 1214447616 | bytes 11142144 | tf_op jit(solution)/shard_map/dot_general | solution.py:135
  352.9 4.0 fusion.10
  358.9 2.8 fusion.22
  363.5 3.6 reshape.151
  367.1 9.0 %scatter_custom_fusion = f32[4096]{0:T(1024)S(1)} fusion(s32[2304]{0:T(1024)S(1)} %fusion.17, f32[2304]{0:T(1024)S(1)} %broadcast.81, f32[]{:T(128)} %constant.22.clone.1), kind=kCustom, calls=%fused_computation.39 | custom fusion | bytes 16388 | tf_op jit(solution)/shard_map/scatter | solution.py:116
  376.7 5.0 %constant_dynamic-slice_fusion = f32[2304,8,1,64]{0,3,2,1:T(8,128)} fusion(f32[2304,8,2,64]{0,3,2,1:T(8,128)} %bitcast.46, s32[]{:T(128)S(6)} %select_n.40), kind=kLoop, calls=%fused_computation.44 | loop fusion | bytes 9437188 | tf_op jit(solution)/shard_map/jit(dynamic_index_in_dim)/dynamic_slice | solution.py:86
  381.8 6.2 %copy.21 = f32[2304,512]{1,0:T(8,128)} copy(f32[2304,512]{0,1:T(8,128)} %bitcast.47) | data formatting | bytes 9437184 | tf_op jit(solution)/shard_map/reshape | solution.py:87
  388.0 3.3 fusion.20
  392.2 23.3 %all-reduce = (f32[4096]{0:T(1024)S(1)}, f32[4096]{0:T(1024)S(1)}, f32[1024]{0:T(1024)S(1)}, f32[1024]{0:T(1024)S(1)}) all-reduce(f32[4096]{0:T(1024)S(1)} %dynamic_update_slice.12, f32[4096]{0:T(1024)S(1)} %dynamic_update_slice.13, ...), channel_id=1, replica_groups=mesh['seq_0'=8,'seq_1'=2,'img_0'=4,'img_1'=2,'fsdp'=2] {'seq_0'}, use_global_device_ids=true, to_apply=%region_7.8 | all-reduce | flops 10240 | bytes 81920 | tf_op jit(solution)/shard_map/psum | solution.py:66
  415.5 5.9 %all-reduce.4 = (f32[4096]{0:T(1024)S(1)}, f32[4096]{0:T(1024)S(1)}, f32[1024]{0:T(1024)S(1)}, f32[1024]{0:T(1024)S(1)}) all-reduce(f32[4096]{0:T(1024)S(1)} %get-tuple-element.8, f32[4096]{0:T(1024)S(1)} %get-tuple-element.9, ...), channel_id=1, replica_groups=mesh['seq_0'=8,'seq_1'=2,'img_0'=4,'img_1'=2,'fsdp'=2] {'seq_1'}, use_global_device_ids=true, to_apply=%region_8.9 | all-reduce | flops 10240 | bytes 81920 | tf_op jit(solution)/shard_map/psum | solution.py:66
  421.4 14.4 %all-reduce.1 = (f32[4096]{0:T(1024)S(1)}, f32[4096]{0:T(1024)S(1)}, f32[1024]{0:T(1024)S(1)}, f32[1024]{0:T(1024)S(1)}) all-reduce(f32[4096]{0:T(1024)S(1)} %get-tuple-element.24, f32[4096]{0:T(1024)S(1)} %get-tuple-element.25, ...), channel_id=1, replica_groups=mesh['seq_0'=8,'seq_1'=2,'img_0'=4,'img_1'=2,'fsdp'=2] {'img_0'}, use_global_device_ids=true, to_apply=%region_9.10 | all-reduce | flops 10240 | bytes 81920 | tf_op jit(solution)/shard_map/psum | solution.py:66
  435.7 10.3 %all-reduce.3 = (f32[4096]{0:T(1024)S(1)}, f32[4096]{0:T(1024)S(1)}, f32[1024]{0:T(1024)S(1)}, f32[1024]{0:T(1024)S(1)}) all-reduce(f32[4096]{0:T(1024)S(1)} %get-tuple-element.12, f32[4096]{0:T(1024)S(1)} %get-tuple-element.13, ...), channel_id=1, replica_groups=mesh['seq_0'=8,'seq_1'=2,'img_0'=4,'img_1'=2,'fsdp'=2] {'img_1'}, use_global_device_ids=true, to_apply=%region_10.11 | all-reduce | flops 10240 | bytes 81920 | tf_op jit(solution)/shard_map/psum | solution.py:66
  446.0 16.1 %all-reduce.2 = (f32[4096]{0:T(1024)}, f32[4096]{0:T(1024)}, f32[1024]{0:T(1024)}, f32[1024]{0:T(1024)}) all-reduce(f32[4096]{0:T(1024)S(1)} %get-tuple-element.20, f32[4096]{0:T(1024)S(1)} %get-tuple-element.21, f32[1024]{0:T(1024)S(1)} %get-tuple-element.22, ...), channel_id=1, replica_groups=mesh['seq_0'=8,'seq_1'=2,'img_0'=4,'img_1'=2,'fsdp'=2] {'fsdp'}, use_global_device_ids=true, to_apply=%region_11.12 | all-reduce | flops 10240 | bytes 81920 | tf_op jit(solution)/shard_map/psum | solution.py:66
  (82 shorter events, 17.1 us)
Async XLA Ops:
  7.2 315.1 %copy-start = (bf16[256,2048]{1,0:T(8,128)(2,1)S(1)}, bf16[256,2048]{1,0:T(8,128)(2,1)}, u32[]{:S(2)}) copy-start(bf16[256,2048]{1,0:T(8,128)(2,1)} %param.14) | copy-start | bytes 3145732
  7.2 44.5 %copy-start.13 = (s32[1,2]{1,0:T(1,128)S(1)}, s32[1,2]{1,0:T(1,128)}, u32[]{:S(2)}) copy-start(s32[1,2]{1,0:T(1,128)} %param.16) | copy-start | bytes 28
  7.2 44.8 %copy-start.9 = (s32[1,2304]{1,0:T(1,128)S(1)}, s32[1,2304]{1,0:T(1,128)}, u32[]{:S(2)}) copy-start(s32[1,2304]{1,0:T(1,128)} %param.17) | copy-start | bytes 27652
  7.2 44.4 %all-gather.9.cloned.1.call-start = ((), (), s32[]{:S(2)}) async-start(), calls=%async_computation.5 | async-start | bytes 3145728 | tf_op jit(solution)/shard_map/all_gather | solution.py:36
  7.9 114.2 %all-gather.7.cloned.1.call-start = ((), (), s32[]{:S(2)}) async-start(), calls=%async_computation.4 | async-start | bytes 4866048 | tf_op jit(solution)/shard_map/all_gather | solution.py:128
  8.7 287.3 %all-gather.11.cloned.1.call-start = ((), (), s32[]{:S(2)}) async-start(), calls=%async_computation.6 | async-start | bytes 18874368 | tf_op jit(solution)/shard_map/all_gather | solution.py:36
  128.9 3.8 copy-start.2
  132.6 1.3 copy-start.10
  132.6 1.3 copy-start.11
  138.7 2.1 copy-start.3
  327.8 9.2 %copy-start.8 = (bf16[512,256]{1,0:T(8,128)(2,1)S(1)}, bf16[512,256]{1,0:T(8,128)(2,1)}, u32[]{:S(2)}) copy-start(bf16[512,256]{1,0:T(8,128)(2,1)} %param.12) | copy-start | bytes 786436
  337.9 8.3 %all-to-all-start.1 = ((bf16[2,512,256]{2,1,0:T(8,128)(2,1)}), bf16[2,512,256]{2,1,0:T(8,128)(2,1)S(1)}, u32[]{:S(2)}, u32[]{:S(2)}) async-start(bf16[2,512,256]{2,1,0:T(8,128)(2,1)} %broadcast_in_dim.7), calls=%async_computation.1 | async-start | bytes 1048576 | tf_op jit(solution)/shard_map/all_to_all | solution.py:19
  341.7 4.5 copy-start.12
  341.7 120.4 %reduce-scatter.2.cloned.1.call-start = ((), (), s32[]{:S(2)}) async-start(), calls=%async_computation.3 | async-start | bytes 2949120 | tf_op jit(solution)/shard_map/reduce_scatter | solution.py:56
  341.7 11.2 %slice-start = ((s8[9437184]{0:T(1024)(128)(4,1)}), s8[1048576]{0:T(1024)(128)(4,1)S(1)}, s32[]{:S(2)}) async-start(s8[9437184]{0:T(1024)(128)(4,1)} %bitcast.44), calls=%async_computation.7 | async-start | bytes 2097152
  346.2 6.7 %copy-start.6 = (bf16[2,512,256]{2,1,0:T(8,128)(2,1)}, bf16[2,512,256]{2,1,0:T(8,128)(2,1)S(1)}, u32[]{:S(2)}) copy-start(bf16[2,512,256]{2,1,0:T(8,128)(2,1)S(1)} %all-to-all-done.1) | copy-start | bytes 1572868
  346.2 6.7 %slice-start.1 = ((s8[9437184]{0:T(1024)(128)(4,1)}), s8[4194304]{0:T(1024)(128)(4,1)S(1)}, s32[]{:S(2)}) async-start(s8[9437184]{0:T(1024)(128)(4,1)} %bitcast.44), calls=%async_computation.8 | async-start | bytes 8388608
  346.2 6.7 %slice-start.2 = ((s8[9437184]{0:T(1024)(128)(4,1)}), s8[4194304]{0:T(1024)(128)(4,1)S(1)}, s32[]{:S(2)}) async-start(s8[9437184]{0:T(1024)(128)(4,1)} %bitcast.44), calls=%async_computation.9 | async-start | bytes 8388608
  367.1 9.1 %copy-start.4 = (bf16[1,256,2048]{2,1,0:T(8,128)(2,1)S(1)}, bf16[1,256,2048]{2,1,0:T(8,128)(2,1)}, u32[]{:S(2)}) copy-start(bf16[1,256,2048]{2,1,0:T(8,128)(2,1)} %param.15) | copy-start | bytes 3145732
  367.1 9.6 %copy-start.7 = (bf16[2,512,256]{2,1,0:T(8,128)(2,1)S(1)}, bf16[2,512,256]{2,1,0:T(8,128)(2,1)}, u32[]{:S(2)}) copy-start(bf16[2,512,256]{2,1,0:T(8,128)(2,1)} %copy-done.6) | copy-start | bytes 1572868
  381.8 6.3 %copy-start.5 = (bf16[2304,256]{1,0:T(8,128)(2,1)S(1)}, bf16[2304,256]{1,0:T(8,128)(2,1)}, u32[]{:S(2)}) copy-start(bf16[2304,256]{1,0:T(8,128)(2,1)} %get-tuple-element.30) | copy-start | bytes 3538948
  388.0 77.3 %copy-start.1 = (bf16[256,2048]{1,0:T(8,128)(2,1)S(1)}, bf16[256,2048]{1,0:T(8,128)(2,1)}, u32[]{:S(2)}) copy-start(bf16[256,2048]{1,0:T(8,128)(2,1)} %param.14) | copy-start | bytes 3145732
Sparse Core Ops, SparseCore 0:
  9.8 41.7 all-gather.8
  53.5 68.5 all-gather.6
  123.9 172.0 all-gather.10
  367.2 79.7 reduce-scatter.1
where the time goes:
time: 473 us; the launch traced here: 472 us
  waiting for transfers between devices  268 us (57%)
  blocking collectives  79.1 us (17%)
  local copies, waits for them, and re-layouts  68.7 us (15%)
  matrix products  22.2 us (5%)
  other arithmetic  16 us (3%)
  between operations  14 us (3%)
    all_gather x2, waiting for transfers between devices, whole_of(): nearer = lax.all_gather(array, axes[-1], axis=dim, tiled=True)  196 us
    all_gather x1, waiting for transfers between devices, per_device(): gathered = lax.all_gather(vision_feats[0], SEQ_FSDP, axis=0, tiled=True)  70 us
    psum x5, blocking collectives, one_axis_at_a_time(): array = lax.psum(array, axis)  69.9 us
    gather x1, local copies, waits for them, and re-layouts, per_device(): picked = whole_grad[abs_pos]  26.2 us
    dot_general x4, matrix products, contract(): lax.dot_general(left, right, (((left_dim,), (right_dim,)), ((), ())), pre...  15.2 us
  transfers between devices with their start and end apart: 5, of which 3 were waited for; matrix products, arithmetic and copies ran while one was open for 10% of the time, Pallas kernels for 0%

commit v1 on v0

v1 whole, which is shorter than its diff:
```python
import jax
import jax.numpy as jnp
from jax import lax
from jax.experimental import pallas as pl
from jax.experimental.pallas import tpu as pltpu
from jax.sharding import Mesh
from jax.sharding import PartitionSpec as P

PATCH = 576
LEN = 2048
SEQ = ("seq_0", "seq_1")
IMG = ("img_0", "img_1")
SEQ_FSDP = ("seq_0", "seq_1", "fsdp")
IMG_FSDP = ("img_0", "img_1", "fsdp")
SEQ_IMG = ("seq_0", "seq_1", "img_0", "img_1")
MESH = pl.DeviceIdType.MESH
BF16 = jnp.bfloat16
F32 = jnp.float32
VMEM = pl.BlockSpec(memory_space=pltpu.VMEM)
DMA = pltpu.SemaphoreType.DMA
LIMIT = 60 * 1024 * 1024


def remote(src, dst, send, recv, device):
    return pltpu.make_async_remote_copy(
        src_ref=src, dst_ref=dst, send_sem=send, recv_sem=recv, device_id=device, device_id_type=MESH
    )


def greet(devices):
    barrier = pltpu.get_barrier_semaphore()
    for device in devices:
        pl.semaphore_signal(barrier, inc=1, device_id=device, device_id_type=MESH)
    pl.semaphore_wait(barrier, len(devices))


def call(kernel, outs, scratch, number, args, flops):
    return pl.pallas_call(
        kernel,
        out_shape=outs,
        in_specs=[VMEM] * len(args),
        out_specs=jax.tree.map(lambda _: VMEM, outs),
        scratch_shapes=scratch,
        compiler_params=pltpu.CompilerParams(
            collective_id=number, has_side_effects=True, vmem_limit_bytes=LIMIT
        ),
        cost_estimate=pl.CostEstimate(flops=flops, bytes_accessed=1 << 20, transcendentals=0),
    )(*args)


def swap_kernel(lm, out, send, recv):
    other = 1 - lax.axis_index("seq_1")
    neighbour = {"seq_1": other}
    greet([neighbour])
    width = out.shape[1]
    columns = pl.ds(pl.multiple_of(other * width, 128), width)
    copy = remote(lm.at[:, columns], out, send, recv, neighbour)
    copy.start()
    copy.wait()


def swap_columns(lm):
    rows, width = lm.shape
    out = jax.ShapeDtypeStruct((rows, width // 2), lm.dtype)
    return call(swap_kernel, out, [DMA, DMA], 0, (lm,), 1 << 30)


def exchange_kernel(v, wo, wi, bi, vs, wos, wis, bis, up_s, up_r, dn_s, dn_r, x_s, x_r, c_s, c_r, w_s, w_r, local):
    layers = vs.shape[0]
    z, xl, c = lax.axis_index("seq_0"), lax.axis_index("seq_1"), lax.axis_index("fsdp")
    other, peer = 1 - xl, 1 - c
    up, down = {"seq_0": (z + 1) % layers}, {"seq_0": (z + layers - 1) % layers}
    across, twin = {"seq_1": other}, {"fsdp": peer}
    greet([up, down, across, twin])
    width = wos.shape[2]
    mine = pl.ds(pl.multiple_of(xl * width, 128), width)
    theirs = pl.ds(pl.multiple_of(other * width, 128), width)
    started = []

    def go(copy):
        copy.start()
        started.append(copy)
        return copy

    n_up, n_down = layers // 2, layers // 2 - 1
    ups = {0: go(remote(v, vs.at[z, xl, c], up_s.at[0], up_r.at[0], up))}
    downs = {0: go(remote(v, vs.at[z, xl, c], dn_s.at[0], dn_r.at[0], down))}
    xs = [go(remote(v, vs.at[z, xl, c], x_s.at[0], x_r.at[0], across))]
    cs = [go(remote(v, vs.at[z, xl, c], c_s.at[0], c_r.at[0], twin))]
    w_x = [
        go(remote(wi, wis.at[c, xl], w_s.at[0], w_r.at[0], across)),
        go(remote(bi, bis.at[xl], w_s.at[1], w_r.at[1], across)),
        go(remote(wo.at[:, theirs], wos.at[xl], w_s.at[2], w_r.at[2], across)),
    ]
    w_c = [go(remote(wi, wis.at[c, xl], w_s.at[3], w_r.at[3], twin))]
    locals_ = [
        pltpu.make_async_copy(v, vs.at[z, xl, c], local.at[0]),
        pltpu.make_async_copy(wo.at[:, mine], wos.at[xl], local.at[1]),
        pltpu.make_async_copy(wi, wis.at[c, xl], local.at[2]),
        pltpu.make_async_copy(bi, bis.at[xl], local.at[3]),
    ]
    for copy in locals_:
        copy.start()
    blocks = [z]

    def arrived(zb):
        j = len(blocks)
        blocks.append(zb)
        xs.append(go(remote(vs.at[zb, xl, c], vs.at[zb, xl, c], x_s.at[j], x_r.at[j], across)))
        cs.append(go(remote(vs.at[zb, xl, c], vs.at[zb, xl, c], c_s.at[j], c_r.at[j], twin)))

    done = 0

    def pass_on(limit):
        nonlocal done
        while done < limit:
            xs[done].wait_recv()
            zb = blocks[done]
            j = layers + done
            cs.append(go(remote(vs.at[zb, other, c], vs.at[zb, other, c], c_s.at[j], c_r.at[j], twin)))
            done += 1

    for s in range(n_up):
        held = len(blocks)
        ups[s].wait_recv()
        zb = (z + layers - 1 - s) % layers
        if s + 1 < n_up:
            ups[s + 1] = go(remote(vs.at[zb, xl, c], vs.at[zb, xl, c], up_s.at[s + 1], up_r.at[s + 1], up))
        arrived(zb)
        if s < n_down:
            downs[s].wait_recv()
            zb = (z + 1 + s) % layers
            if s + 1 < n_down:
                downs[s + 1] = go(
                    remote(vs.at[zb, xl, c], vs.at[zb, xl, c], dn_s.at[s + 1], dn_r.at[s + 1], down)
                )
            arrived(zb)
        pass_on(held)
    w_x[0].wait_recv()
    w_c.append(go(remote(wis.at[c, other], wis.at[c, other], w_s.at[4], w_r.at[4], twin)))
    pass_on(layers)
    for copy in w_x[1:] + w_c + cs:
        copy.wait_recv()
    for copy in started:
        copy.wait_send()
    for copy in locals_:
        copy.wait()


def exchange(v, wo, wi, bi, layers):
    outs = (
        jax.ShapeDtypeStruct((layers, 2, 2, *v.shape), v.dtype),
        jax.ShapeDtypeStruct((2, wo.shape[0], wo.shape[1] // 2), wo.dtype),
        jax.ShapeDtypeStruct((2, 2, *wi.shape), wi.dtype),
        jax.ShapeDtypeStruct((2, *bi.shape), bi.dtype),
    )
    half = layers // 2
    sems = [half, half, half - 1, half - 1, layers, layers, 2 * layers, 2 * layers, 5, 5, 4]
    return call(exchange_kernel, outs, [DMA((n,)) for n in sems], 1, (v, wo, wi, bi), 1 << 33)


CHUNKS = 3


def middle_kernel(hp, slope, wo, pg, ws, r1, keep, give, r2, ry, c_s, c_r, x_s, x_r, y_s, y_r):
    y, xl, c = lax.axis_index("img_0"), lax.axis_index("seq_1"), lax.axis_index("fsdp")
    other, peer = 1 - xl, 1 - c
    ny = wo.shape[1]
    across, twin = {"seq_1": other}, {"fsdp": peer}
    ys = [{"img_0": (y + k) % ny} for k in range(1, ny)]
    greet([across, twin] + ys)
    rows, width = pg.shape
    step = rows // CHUNKS

    def lanes(a, b):
        return pl.ds(pl.multiple_of((a * 2 + b) * width, 128), width)

    firsts, seconds, thirds = [], [], []
    for k in range(CHUNKS):
        part = pl.ds(k * step, step)
        for p in range(2):
            side = other if p == 0 else xl
            copy = remote(hp.at[part, lanes(side, peer)], r1.at[p, part], c_s.at[p, k], c_r.at[p, k], twin)
            copy.start()
            firsts.append(copy)
    for k in range(1, ny):
        copy = remote(wo.at[:, (y + k) % ny], ry.at[k - 1], y_s.at[k - 1], y_r.at[k - 1], ys[k - 1])
        copy.start()
        thirds.append(copy)
    for k in range(CHUNKS):
        part = pl.ds(k * step, step)
        firsts[2 * k].wait_recv()
        give[part, :] = (hp[part, lanes(other, c)].astype(F32) + r1[0, part, :].astype(F32)).astype(BF16)
        copy = remote(give.at[part], r2.at[part], x_s.at[k], x_r.at[k], across)
        copy.start()
        seconds.append(copy)
        firsts[2 * k + 1].wait_recv()
        keep[part, :] = hp[part, lanes(xl, c)].astype(F32) + r1[1, part, :].astype(F32)
    for k in range(CHUNKS):
        part = pl.ds(k * step, step)
        seconds[k].wait_recv()
        pg[part, :] = ((keep[part, :] + r2[part, :].astype(F32)) * slope[part, :]).astype(BF16)
    total = wo[:, y].astype(F32)
    for k in range(1, ny):
        thirds[k - 1].wait_recv()
        total = total + ry[k - 1].astype(F32)
    ws[...] = total.astype(BF16)
    for copy in firsts + seconds + thirds:
        copy.wait_send()


def middle(hp, slope, wo):
    rows, width = slope.shape
    ny = wo.shape[1]
    outs = (
        jax.ShapeDtypeStruct((rows, width), BF16),
        jax.ShapeDtypeStruct((2, *wo.shape[2:]), BF16),
    )
    scratch = [
        pltpu.VMEM((2, rows, width), BF16),
        pltpu.VMEM((rows, width), F32),
        pltpu.VMEM((rows, width), BF16),
        pltpu.VMEM((rows, width), BF16),
        pltpu.VMEM((ny - 1, 2, *wo.shape[2:]), BF16),
        DMA((2, CHUNKS)),
        DMA((2, CHUNKS)),
        DMA((CHUNKS,)),
        DMA((CHUNKS,)),
        DMA((ny - 1,)),
        DMA((ny - 1,)),
    ]
    return call(middle_kernel, outs, scratch, 2, (hp, slope, wo), 1 << 32)


def last_kernel(
    ws, wi, vec, w_out, w_in, gain, bias, b_out, b_in, rx, ri, v1, t1, v2, t2, v3, x_s, x_r, i_s, i_r, a_s, a_r, b_s, b_r, d_s, d_r
):
    layers, ny = v3.shape[0], wi.shape[0]
    z, xl, c = lax.axis_index("seq_0"), lax.axis_index("seq_1"), lax.axis_index("fsdp")
    y, xh = lax.axis_index("img_0"), lax.axis_index("img_1")

    def flip(me, bit):
        return 1 - me if bit else me

    plane = []
    for dy in range(ny):
        for dx in range(2):
            for dc in range(2):
                if (dy, dx, dc) != (0, 0, 0):
                    plane.append((dy, dx, dc))
    plane_ids = [((y + dy) % ny, flip(xh, dx), flip(c, dc)) for dy, dx, dc in plane]
    plane_dev = [{"img_0": a, "img_1": b, "fsdp": d} for a, b, d in plane_ids]
    side_dev = [{"seq_1": 1 - xl}, {"seq_1": 1 - xl, "img_1": 1 - xh}]
    corner = {"seq_1": 1 - xl, "fsdp": 1 - c}
    stack = [{"seq_0": (z + k) % layers} for k in range(1, layers)]
    greet(plane_dev + side_dev + [corner] + stack)
    started = []

    def go(copy):
        copy.start()
        started.append(copy)
        return copy

    stage_a = []
    for n, (dy, dx, dc) in enumerate(plane):
        if dc == 0:
            k = len(stage_a)
            stage_a.append(go(remote(vec, v1.at[k], a_s.at[k], a_r.at[k], plane_dev[n])))
    ins = []
    for n, (dy, dx, dc) in enumerate(plane):
        a, b, d = plane_ids[n]
        ins.append((go(remote(wi.at[a, b, d], ri.at[n], i_s.at[n], i_r.at[n], plane_dev[n])), n, dc))
    outs = [
        (go(remote(ws.at[1 - xl, xh], rx.at[0], x_s.at[0], x_r.at[0], side_dev[0])), 0, 1),
        (go(remote(ws.at[1 - xl, 1 - xh], rx.at[1], x_s.at[1], x_r.at[1], side_dev[1])), 1, 1),
        (go(remote(ws.at[xl, 1 - xh], rx.at[2], x_s.at[2], x_r.at[2], {"img_1": 1 - xh})), 2, 0),
    ]
    total = vec[...]
    for k, copy in enumerate(stage_a):
        copy.wait_recv()
        total = total + v1[k]
    t1[...] = total
    q = xl * 2 + c
    stage_b = []
    for k, (dx, dc) in enumerate(((0, 1), (1, 0), (1, 1))):
        device = {"seq_1": flip(xl, dx), "fsdp": flip(c, dc)}
        stage_b.append(go(remote(t1, v2.at[q], b_s.at[k], b_r.at[k], device)))
    v2[q] = total
    for copy in stage_b:
        copy.wait_recv()
    t2[0:16] = v2[0, 0:16] + v2[1, 0:16] + v2[2, 0:16] + v2[3, 0:16]
    t2[16:32] = v2[0, 16:32] + v2[2, 16:32]
    t2[32:48] = v2[1, 16:32] + v2[3, 16:32]
    for j in range(4):
        t2[48 + j : 49 + j] = v2[j, 32:33]
    t2[52:56] = jnp.zeros((4, 128), F32)
    stage_d = []
    for k in range(1, layers):
        stage_d.append(go(remote(t2, v3.at[z], d_s.at[k - 1], d_r.at[k - 1], stack[k - 1])))
    v3[z] = t2[...]

    same = wi[y, xh, c].astype(F32)
    cross = jnp.zeros_like(same)
    for copy, n, dc in ins:
        copy.wait_recv()
        if dc:
            cross = cross + ri[n].astype(F32)
        else:
            same = same + ri[n].astype(F32)
    width = same.shape[1]
    w_in[:, pl.ds(pl.multiple_of(c * width, 128), width)] = same
    w_in[:, pl.ds(pl.multiple_of((1 - c) * width, 128), width)] = cross
    near = ws[xl, xh].astype(F32)
    outs[2][0].wait_recv()
    near = near + rx[2].astype(F32)
    outs[0][0].wait_recv()
    outs[1][0].wait_recv()
    far = rx[0].astype(F32) + rx[1].astype(F32)
    width = near.shape[1]
    w_out[:, pl.ds(pl.multiple_of(xl * width, 128), width)] = near
    w_out[:, pl.ds(pl.multiple_of((1 - xl) * width, 128), width)] = far

    for copy in stage_d:
        copy.wait_recv()
    total = v3[0]
    for j in range(1, layers):
        total = total + v3[j]
    gain[...] = total[0:8]
    bias[...] = total[8:16]
    b_out[...] = total[16:48]
    for j in range(layers):
        b_in[4 * j : 4 * j + 4, :] = v3[j, 48:52]
    for copy in started:
        copy.wait_send()


def last(ws, wi, vec, layers):
    ny = wi.shape[0]
    members = ny * 4 - 1
    block = wi.shape[3:]
    outs = (
        jax.ShapeDtypeStruct((ws.shape[2], 2 * ws.shape[3]), F32),
        jax.ShapeDtypeStruct((block[0], 2 * block[1]), F32),
        jax.ShapeDtypeStruct((8, 128), F32),
        jax.ShapeDtypeStruct((8, 128), F32),
        jax.ShapeDtypeStruct((32, 128), F32),
        jax.ShapeDtypeStruct((4 * layers, 128), F32),
    )
    scratch = [
        pltpu.VMEM((3, *ws.shape[2:]), BF16),
        pltpu.VMEM((members, *block), BF16),
        pltpu.VMEM((2 * ny - 1, 40, 128), F32),
        pltpu.VMEM((40, 128), F32),
        pltpu.VMEM((4, 40, 128), F32),
        pltpu.VMEM((56, 128), F32),
        pltpu.VMEM((layers, 56, 128), F32),
    ]
    for n in (3, members, 2 * ny - 1, 3, layers - 1):
        scratch += [DMA((n,)), DMA((n,))]
    return call(last_kernel, outs, scratch, 3, (ws, wi, vec), 1 << 32)


def gelu_parts(preact):
    cumul = 0.5 * (1.0 + lax.erf(preact * 0.7071067811865476))
    density = jnp.exp(-0.5 * preact * preact) * 0.3989422804014327
    return (preact * cumul, cumul + preact * density)


def contract(left, right, left_dim, right_dim, out=F32):
    return lax.dot_general(left, right, (((left_dim,), (right_dim,)), ((), ())), preferred_element_type=out)


def per_device(vision_feats, ln_gain, ln_bias, w_in, b_in, w_out, lm_grad, image_counts, token_pos):
    layers = lax.axis_size("seq_0")
    xl, c = lax.axis_index("seq_1"), lax.axis_index("fsdp")
    seq_index = lax.axis_index(SEQ)
    lm = lm_grad[0]
    block_rows, half = lm.shape
    quarter = half // 2
    own_hid = b_in.shape[0]
    unit = own_hid // 2
    layer_hid = 2 * own_hid

    own = lax.dynamic_slice_in_dim(lm, xl * quarter, quarter, 1)
    gathered_a = lax.all_gather(own, "seq_0", axis=0)
    swapped = swap_columns(lax.optimization_barrier((lm, own))[0])
    gathered_b = lax.all_gather(swapped, "seq_0", axis=0)

    counts, positions = image_counts[0], token_pos[0]
    images = positions.shape[0] // PATCH
    starts = []
    for i in range(images):
        starts.append(jnp.where(i >= counts[0], LEN, 0) + positions[i * PATCH])

    v_all, w_out_q, w_in_all, b_in_all = exchange(
        vision_feats[0], w_out, w_in, b_in.reshape(-1, 128), layers
    )
    w_out_q = w_out_q.reshape(layer_hid, quarter)
    w_in_layer = jnp.moveaxis(w_in_all, 1, 2).reshape(-1, layer_hid)
    b_in_layer = b_in_all.reshape(layer_hid)
    values = v_all.reshape(-1, *v_all.shape[3:]).astype(F32)
    row_mean = jnp.mean(values, axis=-1, keepdims=True)
    centred = values - row_mean
    row_var = jnp.mean(centred * centred, axis=-1, keepdims=True)
    normed = centred * lax.rsqrt(row_var + 1e-05)
    rows = normed.shape[0] * normed.shape[1]
    normed_in = (normed * ln_gain + ln_bias).astype(BF16).reshape(rows, -1)
    normed = normed.astype(BF16).reshape(rows, -1)
    preact = contract(normed_in, w_in_layer, 1, 0) + b_in_layer
    hidden = gelu_parts(preact)[0].astype(BF16)
    at = (2 * xl + c) * unit
    slope = gelu_parts(lax.dynamic_slice_in_dim(preact, at, unit, 1))[1]
    w_in_own = lax.dynamic_slice_in_dim(w_in_layer, at, unit, 1).astype(F32)
    hidden_pos = jnp.zeros((layers * 2 * block_rows, layer_hid), BF16)
    for i, start in enumerate(starts):
        hidden_pos = lax.dynamic_update_slice(hidden_pos, hidden[i * PATCH : (i + 1) * PATCH], (start, 0))
    hidden_pos = hidden_pos.reshape(layers, 2, block_rows, layer_hid)

    position = seq_index * block_rows + jnp.arange(block_rows, dtype=jnp.int32)
    taken = sum(((position >= s) & (position < s + PATCH)).astype(BF16) for s in starts)
    out_bias = jnp.dot(taken[None, :], lm, preferred_element_type=F32)[0]

    pa = gathered_a.reshape(-1, quarter)
    pb = gathered_b.reshape(-1, quarter)
    ha = lax.dynamic_index_in_dim(hidden_pos, xl, 1, keepdims=False).reshape(-1, layer_hid)
    hb = lax.dynamic_index_in_dim(hidden_pos, 1 - xl, 1, keepdims=False).reshape(-1, layer_hid)
    part_a = contract(pa, w_out_q, 1, 1, BF16)
    w_part_a = contract(ha, pa, 0, 0)
    part_b = contract(pb, w_out_q, 1, 1, BF16)
    w_part = (w_part_a + contract(hb, pb, 0, 0)).astype(BF16)
    shape = (layers, 1, block_rows, layer_hid)
    hp = jnp.zeros((layers, 2, block_rows, layer_hid), BF16)
    hp = lax.dynamic_update_slice(hp, part_a.reshape(shape), (0, xl, 0, 0))
    hp = lax.dynamic_update_slice(hp, part_b.reshape(shape), (0, 1 - xl, 0, 0)).reshape(-1, layer_hid)
    hp = jnp.concatenate([lax.dynamic_slice_in_dim(hp, s, PATCH, 0) for s in starts], axis=0)

    ny = lax.axis_size("img_0")
    block = layer_hid // (2 * ny)
    pg, w_sum = middle(hp, slope, w_part.reshape(2, ny, block, quarter))
    w_sum = w_sum.reshape(2, 2, block // 2, quarter)
    w_in_part = contract(normed_in, pg, 0, 0, BF16)
    moment = contract(normed, pg, 0, 0)
    b_in_part = jnp.sum(pg.astype(F32), axis=0)
    gain_part = jnp.sum(moment * w_in_own, axis=1)
    bias_part = jnp.sum(w_in_own * b_in_part, axis=1)
    vec = jnp.concatenate([gain_part, bias_part, out_bias, b_in_part, jnp.zeros((7 * 128,), F32)])
    w_out_grad, w_in_grad, gain, bias, b_out, b_in_grad = last(
        w_sum, w_in_part.reshape(ny, 2, 2, -1, unit), vec.reshape(-1, 128), layers
    )
    return (w_in_grad, b_in_grad.reshape(-1), w_out_grad, b_out.reshape(-1), gain.reshape(-1), bias.reshape(-1))


def solution(mesh):
    finer = Mesh(
        mesh.devices.reshape(8, 2, 4, 2, mesh.shape["fsdp"]),
        ("seq_0", "seq_1", "img_0", "img_1", "fsdp"),
    )
    placed = (
        P(IMG, SEQ_FSDP, None),
        P(),
        P(),
        P("fsdp", SEQ),
        P(SEQ),
        P(SEQ, "fsdp"),
        P(IMG, SEQ, "fsdp"),
        P(IMG, None),
        P(IMG, None),
    )
    return jax.shard_map(
        per_device,
        mesh=finer,
        in_specs=placed,
        out_specs=(P(IMG_FSDP, SEQ), P(), P(SEQ_IMG, "fsdp"), P(), P(), P()),
        check_vma=False,
    )
```

time: 473 us -> 237 us (0.50)
  waiting for transfers between devices: 268 us -> 0.06 us
  Pallas kernels: 0 us -> 117 us
  blocking collectives: 79.1 us -> 0 us
  local copies, waits for them, and re-layouts: 68.7 us -> 51.9 us
  other arithmetic: 16 us -> 22.7 us
    all_gather x3 -> x2, waiting for transfers between devices: 266 us -> 0.02 us  [the longest x1 0.02 us: per_device(): gathered_a = lax.all_gather(own, 'seq_0', axis=0)]
    pallas_call x0 -> x4, Pallas kernels: none -> 117 us  [call(): pl.pallas_call(kernel, out_shape=outs, in_specs=[VMEM] * len(args), out_s...]
    psum x5 -> x0, blocking collectives: 69.9 us -> none  [one_axis_at_a_time(): array = lax.psum(array, axis)]
    gather x1 -> x0, local copies, waits for them, and re-layouts: 26.2 us -> none  [per_device(): picked = whole_grad[abs_pos]]
    dynamic_update_slice x4 -> x5, local copies, waits for them, and re-layouts: 0.59 us -> 15.8 us  [the longest x4 15.6 us: per_device(): lax.dynamic_update_slice(hidden_pos, hidden[i * PATCH:(i + 1) * PATCH], (...]
    dot_general x4 -> x7, matrix products: 15.2 us -> 26.5 us  [contract(): lax.dot_general(left, right, (((left_dim,), (right_dim,)), ((), ())), pre...]
    unnamed x34 -> x40, local copies, waits for them, and re-layouts: 2.77 us -> 13.5 us
    convert_element_type x0 -> x2, other arithmetic: none -> 9.83 us  [the longest x1 6.26 us: per_device(): normed = normed.astype(BF16).reshape(rows, -1)]
  transfers between devices with their start and end apart: 5 -> 2, of which waited for: 3 -> 0; matrix products, arithmetic and copies ran while one was open for 10% -> 29% of each run, Pallas kernels for 0% -> 24%
where the time goes in v1:
time: 237 us; the launch traced here: 236 us
  Pallas kernels  117 us (49%)
  local copies, waits for them, and re-layouts  51.9 us (22%)
  matrix products  26.8 us (11%)
  other arithmetic  22.7 us (10%)
  between operations  17.2 us (7%)
    pallas_call x4, Pallas kernels, call(): pl.pallas_call(kernel, out_shape=outs, in_specs=[VMEM] * len(args), out_s...  117 us
    dot_general x7, matrix products, contract(): lax.dot_general(left, right, (((left_dim,), (right_dim,)), ((), ())), pre...  26.5 us
    dynamic_update_slice x4, local copies, waits for them, and re-layouts, per_device(): lax.dynamic_update_slice(hidden_pos, hidden[i * PATCH:(i + 1) * PATCH], (...  15.6 us
    unnamed x40, local copies, waits for them, and re-layouts  13.5 us
    dot_general x1, local copies, waits for them, and re-layouts, contract(): lax.dot_general(left, right, (((left_dim,), (right_dim,)), ((), ())), pre...  6.8 us
    convert_element_type x1, other arithmetic, per_device(): normed = normed.astype(BF16).reshape(rows, -1)  6.26 us
    dynamic_slice x1, local copies, waits for them, and re-layouts, per_device(): lax.dynamic_index_in_dim(hidden_pos, 1 - xl, 1, keepdims=False)  4.78 us
  transfers between devices with their start and end apart: 2, of which 0 were waited for; matrix products, arithmetic and copies ran while one was open for 29% of the time, Pallas kernels for 24%

profile of v1, /device:TPU:1, one launch (start us, length us, event | category | flops | bytes accessed | tf_op | source)
XLA Modules:
  0.0 235.9 jit_solution(15661166661658355089)
XLA Ops:
  7.2 14.7 %shard_map.137 = bf16[256,1024]{1,0:T(8,128)(2,1)} custom-call(bf16[256,2048]{1,0:T(8,128)(2,1)} %bitcast.75), custom_call_target="tpu_custom_call" | custom-call | flops 1073741824 | bytes 1048576 | tf_op jit(solution)/shard_map/pallas_call | solution.py:38
  27.0 57.7 %shard_map.136 = (bf16[8,2,2,72,1024]{4,3,2,1,0:T(8,128)(2,1)}, bf16[2,256,1024]{2,1,0:T(8,128)(2,1)}, bf16[2,2,512,256]{3,2,1,0:T(8,128)(2,1)}, f32[2,2,128]{2,1,0:T(2,128)}) custom-call(bf16[72,1024]{1,0:T(8,128)(2,1)} %bitcast.88, bf16[256,2048]{1,0:T(8,128)(2,1)} %wo.1, bf16[512,256]{1,0:T(8,128)(2,1)} %wi.1, f32[2,128]{1,0:T(2,128)} %bitcast.89), custom_call_target="tpu_custom_call" | custom-call | flops 8589934592 | bytes 1048576 | tf_op jit(solution)/shard_map/pallas_call | solution.py:38
  84.7 2.3 copy.25
  87.3 3.1 %convert_reduce_fusion = f32[8,2,2,72]{3,2,1,0:T(2,128)S(1)} fusion(bf16[8,2,2,72,1024]{4,3,2,1,0:T(8,128)(2,1)} %get-tuple-element.19), kind=kLoop, calls=%fused_computation.5 | loop fusion | flops 4716288 | bytes 4727808 | tf_op jit(solution)/shard_map/reduce_sum | solution.py:402
  90.6 3.8 %multiply_reduce_fusion = f32[8,2,2,72]{3,2,1,0:T(2,128)S(1)} fusion(bf16[8,2,2,72,1024]{4,3,2,1,0:T(8,128)(2,1)} %get-tuple-element.19, f32[8,2,2,72]{3,2,1,0:T(2,128)S(1)} %broadcast_multiply_fusion), kind=kLoop, calls=%fused_computation.4 | loop fusion | flops 9434880 | bytes 4737024 | tf_op jit(solution)/shard_map/reduce_sum | solution.py:404
  94.5 6.3 %fusion.1 = (bf16[2304,1024]{1,0:T(8,128)(2,1)}, bf16[2304,1024]{1,0:T(8,128)(2,1)}) fusion(bf16[8,2,2,72,1024]{4,3,2,1,0:T(8,128)(2,1)} %get-tuple-element.19, f32[2304]{0:T(1024)S(1)} %rsqrt.13, f32[2304]{0:T(1024)S(1)} %div.10, f32[1024]{0:T(1024)S(1)} %copy-done.5, f32[1024]{0:T(1024)S(1)} %copy-done.6), kind=kLoop, calls=%fused_computation.6 | loop fusion | flops 16515072 | bytes 14182400 | tf_op jit(solution)/shard_map/convert_element_type | solution.py:408
  100.8 6.8 %copy.26 = bf16[1024,2304]{1,0:T(8,128)(2,1)} copy(bf16[1024,2304]{0,1:T(8,128)(2,1)} %bitcast.68) | data formatting | bytes 9437184 | tf_op jit(solution)/shard_map/dot_general | solution.py:370
  108.6 3.6 %add_convert_fusion.1 = bf16[8,2,2,72,1024]{4,3,2,1,0:T(8,128)(2,1)S(1)} fusion(bf16[8,2,2,72,1024]{4,3,2,1,0:T(8,128)(2,1)} %get-tuple-element.19, f32[1024]{0:T(1024)S(1)} %copy-done.5, f32[1024]{0:T(1024)S(1)} %copy-done.6, f32[8,2,2,72]{3,2,1,0:T(2,128)S(1)} %add_rsqrt_fusion, f32[8,2,2,72]{3,2,1,0:T(2,128)S(1)} %broadcast_multiply_fusion), kind=kLoop, calls=%fused_computation.3 | loop fusion | flops 14155776 | bytes 9463808 | tf_op jit(solution)/shard_map/convert_element_type | solution.py:407
  112.1 4.6 %multiply_convert_fusion = (bf16[2304,512]{1,0:T(8,128)(2,1)S(1)}, f32[2304,512]{1,0:T(8,128)}) fusion(f32[512]{0:T(512)S(1)} %bitcast.98, bf16[2304,1024]{1,0:T(8,128)(2,1)S(1)} %bitcast.73, bf16[1024,512]{1,0:T(8,128)(2,1)S(1)} %bitcast.79), kind=kOutput, calls=%fused_computation.8 | convolution fusion | flops 2422996992 | bytes 12847104 | tf_op jit(solution)/shard_map/dot_general | solution.py:370
  119.2 3.9 %dynamic_update_slice.20 = bf16[4096,512]{1,0:T(8,128)(2,1)} dynamic-update-slice(bf16[4096,512]{1,0:T(8,128)(2,1)} %broadcast_in_dim.7, bf16[576,512]{1,0:T(8,128)(2,1)S(1)} %get-tuple-element.41, s32[]{:T(128)S(6)} %select_n.53, s32[]{:T(128)} %constant.30.clone.1) | dynamic-update-slice | bytes 1179652 | tf_op jit(solution)/shard_map/dynamic_update_slice | solution.py:416
  123.1 3.9 %dynamic_update_slice.21 = bf16[4096,512]{1,0:T(8,128)(2,1)} dynamic-update-slice(bf16[4096,512]{1,0:T(8,128)(2,1)} %dynamic_update_slice.20, bf16[576,512]{1,0:T(8,128)(2,1)S(1)} %get-tuple-element.40, s32[]{:T(128)S(6)} %select_n.55, s32[]{:T(128)} %constant.30.clone.1) | dynamic-update-slice | bytes 1179652 | tf_op jit(solution)/shard_map/dynamic_update_slice | solution.py:416
  127.0 3.9 %dynamic_update_slice.22 = bf16[4096,512]{1,0:T(8,128)(2,1)} dynamic-update-slice(bf16[4096,512]{1,0:T(8,128)(2,1)} %dynamic_update_slice.21, bf16[576,512]{1,0:T(8,128)(2,1)S(1)} %get-tuple-element.39, s32[]{:T(128)S(6)} %select_n.57, s32[]{:T(128)} %constant.30.clone.1) | dynamic-update-slice | bytes 1179652 | tf_op jit(solution)/shard_map/dynamic_update_slice | solution.py:416
  130.9 3.9 %dynamic_update_slice.23 = bf16[4096,512]{1,0:T(8,128)(2,1)} dynamic-update-slice(bf16[4096,512]{1,0:T(8,128)(2,1)} %dynamic_update_slice.22, bf16[576,512]{1,0:T(8,128)(2,1)S(1)} %get-tuple-element.38, s32[]{:T(128)S(6)} %select_n.59, s32[]{:T(128)} %constant.30.clone.1) | dynamic-update-slice | bytes 1179652 | tf_op jit(solution)/shard_map/dynamic_update_slice | solution.py:416
  134.8 4.8 %constant_dynamic-slice_fusion.1 = (bf16[8,1,256,512]{3,2,1,0:T(8,128)(2,1)}, bf16[8,1,256,512]{3,2,1,0:T(8,128)(2,1)}) fusion(bf16[8,2,256,512]{3,2,1,0:T(8,128)(2,1)} %bitcast.69, s32[]{:T(128)S(6)} %select_n.51, s32[]{:T(128)S(6)} %select_n.50), kind=kLoop, calls=%fused_computation.33 | loop fusion | bytes 8388616 | tf_op jit(solution)/shard_map/jit(dynamic_index_in_dim)/dynamic_slice | solution.py:426
  139.8 2.7 %fusion.5.slope = f32[2304,128]{1,0:T(8,128)} fusion(f32[2304,512]{1,0:T(8,128)} %get-tuple-element.47, s32[]{:T(128)S(6)} %select_n.60), kind=kLoop, calls=%fused_computation.18 | loop fusion | flops 2359296 | bytes 2359300 | tf_op jit(solution)/shard_map/add | solution.py:366
  142.5 5.9 %convolution_bitcast_fusion = bf16[2048,512]{0,1:T(8,128)(2,1)} fusion(bf16[512,1024]{1,0:T(8,128)(2,1)S(1)} %bitcast.94, bf16[2048,1024]{1,0:T(8,128)(2,1)} %all-gather.6.cloned.1.call-done), kind=kOutput, calls=%fused_computation.9 | convolution fusion | flops 2147483648 | bytes 7340032 | tf_op jit(solution)/shard_map/dot_general | solution.py:370
  148.4 2.9 %copy.29 = bf16[2048,512]{1,0:T(8,128)(2,1)S(1)} copy(bf16[2048,512]{0,1:T(8,128)(2,1)} %convolution_bitcast_fusion) | data formatting | bytes 4194304 | tf_op jit(solution)/shard_map/reshape | solution.py:434
  153.6 2.5 %bitcast_dynamic-update-slice_fusion = bf16[8,2,256,512]{3,2,1,0:T(8,128)(2,1)S(1)} fusion(bf16[8,2,256,512]{3,2,1,0:T(8,128)(2,1)S(1)} %broadcast_in_dim.6, s32[]{:T(128)S(6)} %select_n.50, bf16[8,256,1024]{2,1,0:T(8,128)(2,1)S(1)} %copy-done.9, bf16[512,1024,1]{1,0,2:T(8,128)(2,1)S(1)} %bitcast.95), kind=kOutput, calls=%fused_computation.11 | convolution fusion | flops 2147483648 | bytes 7340036 | tf_op jit(solution)/shard_map/dot_general | solution.py:370
  157.7 2.4 %fusion.17 = f32[512,1024]{1,0:T(8,128)S(1)} fusion(bf16[2048,512]{1,0:T(8,128)(2,1)S(1)} %bitcast.77, bf16[2048,1024]{1,0:T(8,128)(2,1)S(1)} %bitcast.87), kind=kOutput, calls=%fused_computation.53 | convolution fusion | flops 2147483648 | bytes 8388608 | tf_op jit(solution)/shard_map/dot_general | solution.py:370
  162.5 3.4 %add_convert_fusion.2 = bf16[512,1024]{1,0:T(8,128)(2,1)} fusion(f32[512,1024]{1,0:T(8,128)S(1)} %fusion.17, bf16[2048,512]{1,0:T(8,128)(2,1)S(1)} %bitcast.76, bf16[2048,1024]{1,0:T(8,128)(2,1)S(1)} %copy-done.8), kind=kOutput, calls=%fused_computation.12 | convolution fusion | flops 2148532224 | bytes 9437184 | tf_op jit(solution)/shard_map/dot_general | solution.py:370
  165.9 21.9 %shard_map.138 = (bf16[2304,128]{1,0:T(8,128)(2,1)}, bf16[2,64,1024]{2,1,0:T(8,128)(2,1)}) custom-call(bf16[2304,512]{1,0:T(8,128)(2,1)} %pad_maximum_fusion.hp, f32[2304,128]{1,0:T(8,128)} %fusion.5.slope, bf16[2,4,64,1024]{3,2,1,0:T(8,128)(2,1)} %bitcast.96), custom_call_target="tpu_custom_call" | custom-call | flops 4294967296 | bytes 1048576 | tf_op jit(solution)/shard_map/pallas_call | solution.py:38
  189.2 4.6 %fusion.7.wi = bf16[4,2,2,64,128]{4,3,2,1,0:T(8,128)(2,1)} fusion(bf16[4,2,2,64,2304]{4,3,2,1,0:T(8,128)(2,1)} %bitcast.72, bf16[2304,128]{1,0:T(8,128)(2,1)} %get-tuple-element.23), kind=kOutput, calls=%fused_computation.22 | convolution fusion | flops 603979776 | bytes 5570560 | tf_op jit(solution)/shard_map/dot_general | solution.py:370
  193.8 3.2 %fusion.6 = f32[1024]{0:T(1024)S(1)} fusion(bf16[2304,1024]{1,0:T(8,128)(2,1)} %get-tuple-element.30, bf16[2304,128]{1,0:T(8,128)(2,1)S(1)} %copy-done.4, bf16[1024,128]{0,1:T(8,128)(2,1)S(1)} %copy-done.3), kind=kOutput, calls=%fused_computation.20 | convolution fusion | flops 604371968 | bytes 5574656 | tf_op jit(solution)/shard_map/dot_general | solution.py:370
  197.8 22.9 %shard_map.139 = (f32[32,2048]{1,0:T(8,128)}, f32[64,256]{1,0:T(8,128)}, f32[8,128]{1,0:T(8,128)}, f32[8,128]{1,0:T(8,128)}, f32[32,128]{1,0:T(8,128)}, /*index=5*/f32[32,128]{1,0:T(8,128)}) custom-call(bf16[2,2,32,1024]{3,2,1,0:T(8,128)(2,1)} %bitcast.97, bf16[4,2,2,64,128]{4,3,2,1,0:T(8,128)(2,1)} %fusion.7.wi, f32[40,128]{1,0:T(8,128)} %bitcast.86), custom_call_target="tpu_custom_call" | custom-call | flops 4294967296 | bytes 1048576 | tf_op jit(solution)/shard_map/pallas_call | solution.py:38
  (65 shorter events, 23.0 us)
Async XLA Ops:
  7.2 14.9 %copy-start = (bf16[1,256,2048]{2,1,0:T(8,128)(2,1)S(1)}, bf16[1,256,2048]{2,1,0:T(8,128)(2,1)}, u32[]{:S(2)}) copy-start(bf16[1,256,2048]{2,1,0:T(8,128)(2,1)} %param.15) | copy-start | bytes 3145732
  7.2 15.8 %copy-start.10 = (s32[1,2]{1,0:T(1,128)S(1)}, s32[1,2]{1,0:T(1,128)}, u32[]{:S(2)}) copy-start(s32[1,2]{1,0:T(1,128)} %param.16) | copy-start | bytes 28
  7.2 135.3 %all-gather.6.cloned.1.call-start = ((), (), s32[]{:S(2)}) async-start(), calls=%async_computation.1 | async-start | bytes 4718592 | tf_op jit(solution)/shard_map/all_gather | solution.py:387
  22.0 129.4 %all-gather.4.cloned.1.call-start = ((), (), s32[]{:S(2)}) async-start(), calls=%async_computation | async-start | bytes 4718592 | tf_op jit(solution)/shard_map/all_gather | solution.py:385
  87.3 7.2 %copy-start.5 = (f32[1024]{0:T(1024)S(1)}, f32[1024]{0:T(1024)}, u32[]{:S(2)}) copy-start(f32[1024]{0:T(1024)} %param.11) | copy-start | bytes 12292
  87.3 7.2 %copy-start.6 = (f32[1024]{0:T(1024)S(1)}, f32[1024]{0:T(1024)}, u32[]{:S(2)}) copy-start(f32[1024]{0:T(1024)} %param.10) | copy-start | bytes 12292
  108.5 3.6 %copy-start.13 = (f32[2,2,128]{2,1,0:T(2,128)S(1)}, f32[2,2,128]{2,1,0:T(2,128)}, u32[]{:S(2)}) copy-start(f32[2,2,128]{2,1,0:T(2,128)} %get-tuple-element.21) | copy-start | bytes 6148
  134.8 7.8 %copy-start.11 = (bf16[2,256,1024]{2,1,0:T(8,128)(2,1)S(1)}, bf16[2,256,1024]{2,1,0:T(8,128)(2,1)}, u32[]{:S(2)}) copy-start(bf16[2,256,1024]{2,1,0:T(8,128)(2,1)} %get-tuple-element.18) | copy-start | bytes 3145732
  148.4 3.4 %copy-start.12 = (bf16[2,256,1024]{2,1,0:T(8,128)(2,1)S(1)}, bf16[2,256,1024]{2,1,0:T(8,128)(2,1)}, u32[]{:S(2)}) copy-start(bf16[2,256,1024]{2,1,0:T(8,128)(2,1)} %get-tuple-element.18) | copy-start | bytes 3145732
  151.4 2.2 copy-start.9
  156.1 1.6 copy-start.2
  157.7 4.0 %copy-start.8 = (bf16[2048,1024]{1,0:T(8,128)(2,1)S(1)}, bf16[2048,1024]{1,0:T(8,128)(2,1)}, u32[]{:S(2)}) copy-start(bf16[2048,1024]{1,0:T(8,128)(2,1)} %all-gather.6.cloned.1.call-done) | copy-start | bytes 12582916
  160.0 2.4 %copy-start.1 = (bf16[8,1,256,512]{3,2,1,0:T(8,128)(2,1)S(1)}, bf16[8,1,256,512]{3,2,1,0:T(8,128)(2,1)}, u32[]{:S(2)}) copy-start(bf16[8,1,256,512]{3,2,1,0:T(8,128)(2,1)} %get-tuple-element.32) | copy-start | bytes 6291460
  187.7 6.1 %copy-start.3 = (bf16[1024,128]{0,1:T(8,128)(2,1)S(1)}, bf16[1024,128]{0,1:T(8,128)(2,1)}, u32[]{:S(2)}) copy-start(bf16[1024,128]{0,1:T(8,128)(2,1)} %copy.30) | copy-start | bytes 786436
  187.8 6.0 %copy-start.4 = (bf16[2304,128]{1,0:T(8,128)(2,1)S(1)}, bf16[2304,128]{1,0:T(8,128)(2,1)}, u32[]{:S(2)}) copy-start(bf16[2304,128]{1,0:T(8,128)(2,1)} %get-tuple-element.23) | copy-start | bytes 1769476
  197.2 0.6 copy-start.7
Sparse Core Ops, SparseCore 0:
  22.1 68.2 all-gather.5
  92.2 52.9 all-gather.3

commit v2 on v1

v2 whole, which is shorter than its diff:
```python
import jax
import jax.numpy as jnp
from jax import lax
from jax.experimental import pallas as pl
from jax.experimental.pallas import tpu as pltpu
from jax.sharding import Mesh
from jax.sharding import PartitionSpec as P

PATCH = 576
LEN = 2048
SEQ = ("seq_0", "seq_1")
IMG = ("img_0", "img_1")
SEQ_FSDP = ("seq_0", "seq_1", "fsdp")
IMG_FSDP = ("img_0", "img_1", "fsdp")
SEQ_IMG = ("seq_0", "seq_1", "img_0", "img_1")
MESH = pl.DeviceIdType.MESH
BF16 = jnp.bfloat16
F32 = jnp.float32
VMEM = pl.BlockSpec(memory_space=pltpu.VMEM)
SMEM = pl.BlockSpec(memory_space=pltpu.SMEM)
ANY = pl.BlockSpec(memory_space=pl.ANY)
DMA = pltpu.SemaphoreType.DMA
LIMIT = 63 * 1024 * 1024
WINDOW = 640


def remote(src, dst, send, recv, device):
    return pltpu.make_async_remote_copy(
        src_ref=src, dst_ref=dst, send_sem=send, recv_sem=recv, device_id=device, device_id_type=MESH
    )


def greet(devices):
    barrier = pltpu.get_barrier_semaphore()
    for device in devices:
        pl.semaphore_signal(barrier, inc=1, device_id=device, device_id_type=MESH)
    pl.semaphore_wait(barrier, len(devices))


def call(kernel, outs, scratch, number, args, flops, specs=None):
    ins, results = specs or ([VMEM] * len(args), [VMEM] * len(outs))
    return pl.pallas_call(
        kernel,
        out_shape=tuple(outs),
        in_specs=ins,
        out_specs=tuple(results),
        scratch_shapes=scratch,
        compiler_params=pltpu.CompilerParams(
            collective_id=number, has_side_effects=number is not None, vmem_limit_bytes=LIMIT
        ),
        cost_estimate=pl.CostEstimate(flops=flops, bytes_accessed=1 << 20, transcendentals=0),
    )(*args)


def gelu_parts(preact):
    cumul = 0.5 * (1.0 + lax.erf(preact * 0.7071067811865476))
    density = jnp.exp(-0.5 * preact * preact) * 0.3989422804014327
    return (preact * cumul, cumul + preact * density)


def contract(left, right, left_dim, right_dim):
    return lax.dot_general(left, right, (((left_dim,), (right_dim,)), ((), ())), preferred_element_type=F32)


def image_starts(counts, token_pos):
    images = token_pos.shape[1] // PATCH
    return [jnp.where(counts[0, 0] <= i, LEN, 0) + token_pos[0, i * PATCH] for i in range(images)]


def main_kernel(
    counts, token_pos, v, wo, wi, bi, lm, gain, bias,
    grads_out, hid_out, slope_out, nrm_out, nin_out, hg_out, turned, b_out,
    grads, vs, wq, wis, bis, mine, r1, give, r2, hg, nrm, nin, hid, slope, pre, nf,
    vu_s, vu_r, vd_s, vd_r, vx_s, vx_r, vc_s, vc_r,
    pu_s, pu_r, pd_s, pd_r, px_s, px_r, wx_s, wx_r, wc_s, wc_r,
    h1_s, h1_r, h2_s, h2_r, local, put_p, put_v, put_h,
):
    layers = vs.shape[0]
    block_rows = lm.shape[0]
    chunk = block_rows // 2
    quarter = grads.shape[1]
    own_hid = wo.shape[0]
    unit = own_hid // 2
    layer_rows = 4 * v.shape[0]
    z, xl, c = lax.axis_index("seq_0"), lax.axis_index("seq_1"), lax.axis_index("fsdp")
    other, peer = 1 - xl, 1 - c
    up, down = {"seq_0": (z + 1) % layers}, {"seq_0": (z + layers - 1) % layers}
    across, twin = {"seq_1": other}, {"fsdp": peer}
    mine_cols = pl.ds(pl.multiple_of(xl * quarter, 128), quarter)
    their_cols = pl.ds(pl.multiple_of(other * quarter, 128), quarter)

    def below(s):
        return (z + layers - s) % layers

    def above(s):
        return (z + s) % layers

    def rows(zb, xq, k):
        return pl.ds(pl.multiple_of((zb * 2 + xq) * block_rows + k * chunk, 128), chunk)

    def ring_p(s, t, upward):
        xq = xl if t == 0 else other
        if upward:
            r = rows(below(s), xq, 0)
            return lambda n: remote(grads.at[r], grads.at[r], pu_s.at[n, t], pu_r.at[n, t], up)
        r = rows(above(s), xq, 1)
        return lambda n: remote(grads.at[r], grads.at[r], pd_s.at[n, t], pd_r.at[n, t], down)

    def ring_v(s, upward):
        zb = below(s) if upward else above(s)
        ref = vs.at[zb, xl, c]
        if upward:
            return lambda n: remote(ref, ref, vu_s.at[n], vu_r.at[n], up)
        return lambda n: remote(ref, ref, vd_s.at[n], vd_r.at[n], down)

    def v_across(s, d, xq):
        ref = vs.at[below(s) if d == 0 else above(s), xq, c]
        return remote(ref, ref, vx_s.at[d, s], vx_r.at[d, s], across)

    def v_twin(s, d, xq, t, cq):
        ref = vs.at[below(s) if d == 0 else above(s), xq, cq]
        return remote(ref, ref, vc_s.at[t, d, s], vc_r.at[t, d, s], twin)

    def p_swap(k, xq):
        r = rows(z, xq, k)
        source = lm.at[pl.ds(k * chunk, chunk), their_cols]
        return remote(source, grads.at[r], px_s.at[k], px_r.at[k], across)

    def w_in_at(cq, xq):
        size = wi.shape[0]
        return wis.at[pl.ds(pl.multiple_of(cq * size, 128), size), pl.ds(pl.multiple_of(xq * own_hid, 128), own_hid)]

    def w_out_at(xq):
        return wq.at[pl.ds(pl.multiple_of(xq * own_hid, 128), own_hid)]

    def w_swap(n, xq):
        source = (wo.at[:, their_cols], wi, bi)[n]
        target = (w_out_at(xq), w_in_at(c, xq), bis.at[xq])[n]
        return remote(source, target, wx_s.at[n], wx_r.at[n], across)

    def w_twin(t, cq):
        ref = w_in_at(cq, xl if t == 0 else other)
        return remote(ref, ref, wc_s.at[t], wc_r.at[t], twin)

    def lanes(xq, cq):
        return pl.ds(pl.multiple_of((xq * 2 + cq) * unit, 128), unit)

    def h_twin(s, xq):
        return remote(mine.at[s, :, :, lanes(xq, peer)], r1.at[s, xq], h1_s.at[s, xq], h1_r.at[s, xq], twin)

    def h_across(s):
        return remote(give.at[s], r2.at[s], h2_s.at[s], h2_r.at[s], across)

    greet([up, down, across, twin])
    locals_ = [
        pltpu.make_async_copy(lm.at[pl.ds(0, chunk), mine_cols], grads.at[rows(z, xl, 0)], local.at[0]),
        pltpu.make_async_copy(lm.at[pl.ds(chunk, chunk), mine_cols], grads.at[rows(z, xl, 1)], local.at[1]),
        pltpu.make_async_copy(v, vs.at[z, xl, c], local.at[2]),
        pltpu.make_async_copy(wo.at[:, mine_cols], w_out_at(xl), local.at[3]),
        pltpu.make_async_copy(wi, w_in_at(c, xl), local.at[4]),
        pltpu.make_async_copy(bi, bis.at[xl], local.at[5]),
    ]
    for copy in locals_:
        copy.start()
    p_swap(0, xl).start()
    p_swap(1, xl).start()
    for n in range(3):
        w_swap(n, xl).start()
    locals_[2].wait()
    ring_v(0, True)(0).start()
    ring_v(0, False)(0).start()
    for copy in locals_[:2]:
        copy.wait()
    ring_p(0, 0, True)(0).start()
    ring_p(0, 0, False)(0).start()
    v_across(0, 0, xl).start()
    v_twin(0, 0, xl, 0, c).start()
    for copy in locals_[3:]:
        copy.wait()
    w_twin(0, c).start()

    starts = image_starts(counts, token_pos)
    here = (z * 2 + xl) * block_rows + lax.broadcasted_iota(jnp.int32, (block_rows, 1), 0)
    taken = jnp.zeros((block_rows, 1), F32)
    for start in starts:
        taken = taken + jnp.where((here >= start) & (here < start + PATCH), 1.0, 0.0)
    for j in range(lm.shape[1] // 128):
        column = lm[:, j * 128 : (j + 1) * 128].astype(F32) * taken
        b_out[j : j + 1, :] = jnp.sum(column, axis=0, keepdims=True)
    def put_chunk(s, t, upward):
        r = rows(below(s) if upward else above(s), xl if t == 0 else other, 0 if upward else 1)
        return pltpu.make_async_copy(grads.at[r], grads_out.at[r], put_p.at[s, t, 0 if upward else 1])

    def put_layer(s, d, n):
        r = pl.ds(pl.multiple_of((below(s) if d == 0 else above(s)) * layer_rows, 32), layer_rows)
        source = (hid, slope, nrm, nin)[n]
        target = (hid_out, slope_out, nrm_out, nin_out)[n]
        return pltpu.make_async_copy(source.at[r], target.at[r], put_v.at[s, d, n])

    def put_sum(s, xq, k):
        r = rows(below(s) if k == 0 else above(s), xq, k)
        return pltpu.make_async_copy(hg.at[r], hg_out.at[r], put_h.at[s, xq, k])

    put_chunk(0, 0, True).start()
    put_chunk(0, 0, False).start()
    p_swap(0, other).wait_recv()
    ring_p(0, 1, True)(0).start()
    put_chunk(0, 1, True).start()
    p_swap(1, other).wait_recv()
    ring_p(0, 1, False)(0).start()
    put_chunk(0, 1, False).start()

    def multiply(s):
        for xq in range(2):
            for k in range(2):
                r = rows(below(s) if k == 0 else above(s), xq, k)
                mine[s, xq * 2 + k] = contract(grads[r, :], wq[...], 1, 1)
        for xq in range(2):
            h_twin(s, xq).start()

    def add_twin(s):
        for xq in range(2):
            h_twin(s, xq).wait_recv()
        give[s] = (mine[s, :, :, lanes(other, c)] + r1[s, other]).astype(BF16)
        h_across(s).start()
        for xq in range(2):
            for k in range(2):
                r = rows(below(s) if k == 0 else above(s), xq, k)
                n = xq * 2 + k
                hg[r, :] = mine[s, n, :, lanes(xl, c)] + r1[s, xl, n]

    def add_across(s):
        h_across(s).wait_recv()
        for xq in range(2):
            for k in range(2):
                r = rows(below(s) if k == 0 else above(s), xq, k)
                hg[r, :] = hg[r, :] + r2[s, xq * 2 + k].astype(F32)
                put_sum(s, xq, k).start()

    def span(body, lo, hi):
        def step(s, carry):
            body(s)
            return carry

        lax.fori_loop(lo, hi, step, 0)

    def normalise(zb):
        for n in range(4):
            values = vs[zb, n // 2, n % 2].astype(F32)
            mean = jnp.mean(values, axis=1, keepdims=True)
            centred = values - mean
            var = jnp.mean(centred * centred, axis=1, keepdims=True)
            size = values.shape[0]
            nf[n * size : (n + 1) * size, :] = centred * lax.rsqrt(var + 1e-05)
        r = pl.ds(pl.multiple_of(zb * layer_rows, 32), layer_rows)
        normed = nf[...]
        nrm[r, :] = normed.astype(BF16)
        nin[r, :] = (normed * gain[...] + bias[...]).astype(BF16)
        pre[...] = contract(nin[r, :], wis[...], 1, 0)
        for xq in range(2):
            for half in range(2):
                at = xq * own_hid + half * unit
                pre[:, at : at + unit] = pre[:, at : at + unit] + bis[xq, half : half + 1, :]
        hid[r, :] = gelu_parts(pre[...])[0].astype(BF16)
        slope[r, :] = gelu_parts(pre[:, lanes(xl, c)])[1]

    v_up, v_down = layers // 2, layers // 2 - 1

    def serve_v(s):
        @pl.when(s <= v_up)
        def _():
            ring_v(s, True)(s - 1).wait_recv()

            @pl.when(s < v_up)
            def _():
                ring_v(s, True)(s).start()

            v_across(s, 0, xl).start()
            v_twin(s, 0, xl, 0, c).start()

        @pl.when(s <= v_down)
        def _():
            ring_v(s, False)(s - 1).wait_recv()

            @pl.when(s < v_down)
            def _():
                ring_v(s, False)(s).start()

            v_across(s, 1, xl).start()
            v_twin(s, 1, xl, 0, c).start()

        @pl.when(s - 1 <= v_up)
        def _():
            v_across(s - 1, 0, other).wait_recv()
            v_twin(s - 1, 0, other, 1, c).start()

        @pl.when((s >= 2) & (s - 1 <= v_down))
        def _():
            v_across(s - 1, 1, other).wait_recv()
            v_twin(s - 1, 1, other, 1, c).start()

    def serve_p(s, t):
        for upward in (True, False):
            ring_p(s, t, upward)(s - 1).wait_recv()

            @pl.when(s < layers - 1)
            def _():
                ring_p(s, t, upward)(s).start()

            put_chunk(s, t, upward).start()

    def use_v(s):
        @pl.when(s <= v_up)
        def _():
            v_twin(s, 0, xl, 0, peer).wait_recv()
            v_twin(s, 0, other, 1, peer).wait_recv()
            normalise(below(s))
            for n in range(4):
                put_layer(s, 0, n).start()

        @pl.when((s >= 1) & (s <= v_down))
        def _():
            v_twin(s, 1, xl, 0, peer).wait_recv()
            v_twin(s, 1, other, 1, peer).wait_recv()
            normalise(above(s))
            for n in range(4):
                put_layer(s, 1, n).start()

    def count(s):
        return jnp.maximum(jnp.minimum(2 * s - 3, s), 0)

    def step(s, carry):
        serve_v(s)
        serve_p(s, 0)

        @pl.when(s == 1)
        def _():
            w_swap(1, other).wait_recv()
            w_twin(1, c).start()

        @pl.when(s == 2)
        def _():
            w_swap(0, other).wait_recv()
            w_swap(2, other).wait_recv()
            for t in range(2):
                w_twin(t, peer).wait_recv()
            turned[...] = wis[:, lanes(xl, c)].astype(F32).T

        span(add_across, count(s - 3), count(s - 2))
        span(add_twin, count(s - 2), count(s - 1))
        span(multiply, count(s - 1), count(s))
        serve_p(s, 1)

        @pl.when(s >= 3)
        def _():
            use_v(s - 3)

        return carry

    lax.fori_loop(1, layers, step, 0)
    span(multiply, layers - 1, layers)
    span(add_twin, layers - 2, layers)
    span(add_across, layers - 3, layers)

    for k in range(2):
        p_swap(k, xl).wait_send()
    for n in range(3):
        w_swap(n, xl).wait_send()
    for t in range(2):
        w_twin(t, c).wait_send()

    def sent_p(s, carry):
        for t in range(2):
            for upward in (True, False):
                ring_p(s, t, upward)(s).wait_send()
        return carry

    lax.fori_loop(0, layers - 1, sent_p, 0)

    def put_done(s, carry):
        for t in range(2):
            for k in range(2):
                put_chunk(s, t, k == 0).wait()
                put_sum(s, t, k).wait()
        return carry

    lax.fori_loop(0, layers, put_done, 0)
    def sent_h(s):
        for xq in range(2):
            h_twin(s, xq).wait_send()
        h_across(s).wait_send()

    span(sent_h, 0, layers)
    for s in range(v_up):
        ring_v(s, True)(s).wait_send()
    for s in range(v_down):
        ring_v(s, False)(s).wait_send()
    for s in range(v_up + 1):
        for d in range(2):
            if d == 0 or 1 <= s <= v_down:
                for n in range(4):
                    put_layer(s, d, n).wait()
                v_across(s, d, xl).wait_send()
                v_twin(s, d, xl, 0, c).wait_send()
                v_twin(s, d, other, 1, c).wait_send()


def main(counts, token_pos, v, wo, wi, bi, lm, gain, bias, layers):
    rows, width = lm.shape
    quarter = width // 2
    own = wo.shape[0]
    unit = own // 2
    hid = 2 * own
    tokens = token_pos.shape[1]
    features = v.shape[1]
    layer_rows = 4 * v.shape[0]
    chunk = rows // 2
    places = layers * 2 * rows
    shapes = [
        ((places, quarter), BF16),
        ((tokens, hid), BF16),
        ((tokens, unit), F32),
        ((tokens, features), BF16),
        ((tokens, features), BF16),
        ((places, unit), F32),
    ]
    outs = [jax.ShapeDtypeStruct(*shape) for shape in shapes]
    outs += [jax.ShapeDtypeStruct((unit, features), F32), jax.ShapeDtypeStruct((width // 128, 128), F32)]
    scratch = [
        pltpu.VMEM((places, quarter), BF16),
        pltpu.VMEM((layers, 2, 2, *v.shape), BF16),
        pltpu.VMEM((hid, quarter), BF16),
        pltpu.VMEM((features, hid), BF16),
        pltpu.VMEM((2, *bi.shape), F32),
        pltpu.VMEM((layers, 4, chunk, hid), F32),
        pltpu.VMEM((layers, 2, 4, chunk, unit), F32),
        pltpu.VMEM((layers, 4, chunk, unit), BF16),
        pltpu.VMEM((layers, 4, chunk, unit), BF16),
        pltpu.VMEM((places, unit), F32),
        pltpu.VMEM((tokens, features), BF16),
        pltpu.VMEM((tokens, features), BF16),
        pltpu.VMEM((tokens, hid), BF16),
        pltpu.VMEM((tokens, unit), F32),
        pltpu.VMEM((layer_rows, hid), F32),
        pltpu.VMEM((layer_rows, features), F32),
    ]
    half = layers // 2
    sems = [(half,), (half - 1,), (2, half + 1), (2, 2, half + 1), (layers - 1, 2), (layers - 1, 2), (2,), (3,), (2,)]
    sems += [(layers, 2), (layers,)]
    for shape in sems:
        scratch += [DMA(shape), DMA(shape)]
    scratch += [DMA((6,)), DMA((layers, 2, 2)), DMA((half + 1, 2, 4)), DMA((layers, 2, 2))]
    specs = [SMEM] * 2 + [VMEM] * 7, [ANY] * 6 + [VMEM] * 2
    return call(main_kernel, outs, scratch, 0, (counts, token_pos, v, wo, wi, bi, lm, gain, bias), 1 << 34, specs)


def product_kernel(
    counts, token_pos, grads, hid, slope, nrm, nin, hg, turned, b_out,
    w_out_part, w_in_part, vec,
    pw, hv, hw, sv, rv, nv, acc, shift, pgs, got, got_p, got_h,
):
    starts = image_starts(counts, token_pos)
    size = PATCH + 8
    places = grads.shape[0]
    windows, sums, bases, lows = [], [], [], []
    for i, start in enumerate(starts):
        base = jnp.minimum((start // 16) * 16, places - WINDOW)
        low = jnp.minimum((start // 8) * 8, places - size)
        bases.append(base)
        lows.append(low)
        windows.append(
            pltpu.make_async_copy(grads.at[pl.ds(pl.multiple_of(base, 16), WINDOW)], pw.at[i], got_p.at[i])
        )
        sums.append(pltpu.make_async_copy(hg.at[pl.ds(pl.multiple_of(low, 8), size)], hw.at[i], got_h.at[i]))
    others = [pltpu.make_async_copy(a, b, got.at[n]) for n, (a, b) in enumerate(((hid, hv), (slope, sv), (nin, rv), (nrm, nv)))]
    for copy in [others[0], windows[0], others[1]] + sums + windows[1:] + others[2:]:
        copy.start()
    shift[PATCH:, :] = jnp.zeros((WINDOW - PATCH, shift.shape[1]), F32)
    vec[16:32, :] = b_out[...]
    vec[33:40, :] = jnp.zeros((7, 128), F32)
    others[0].wait()
    for i, start in enumerate(starts):
        shift[0:PATCH, :] = hv[i * PATCH : (i + 1) * PATCH, :].astype(F32)
        left = pltpu.roll(shift[...], start - bases[i], 0).astype(BF16)
        windows[i].wait()
        product = contract(left, pw[i], 0, 0)
        acc[...] = product if i == 0 else acc[...] + product
    w_out_part[...] = acc[...].astype(BF16)
    unit = sv.shape[1]
    total = jnp.zeros((1, unit), F32)
    others[1].wait()
    for i, start in enumerate(starts):
        r = slice(i * PATCH, (i + 1) * PATCH)
        sums[i].wait()
        back = jnp.where(start == lows[i], 0, size - (start - lows[i]))
        window = pltpu.roll(hw[i], back, 0)[0:PATCH]
        pg = (window * sv[r, :]).astype(BF16)
        pgs[r, :] = pg
        total = total + jnp.sum(pg.astype(F32), axis=0, keepdims=True)
    vec[32:33, :] = total
    others[2].wait()
    w_in_part[...] = contract(pgs[...], rv[...], 0, 0).T
    others[3].wait()
    moment = contract(pgs[...], nv[...], 0, 0)
    column = contract(pgs[...], jnp.ones((pgs.shape[0], 128), BF16), 0, 0)
    for j in range(nv.shape[1] // 128):
        at = slice(j * 128, (j + 1) * 128)
        vec[j : j + 1, :] = jnp.sum(moment[:, at] * turned[:, at], axis=0, keepdims=True)
        vec[8 + j : 9 + j, :] = jnp.sum(column * turned[:, at], axis=0, keepdims=True)


def products(counts, token_pos, grads, hid, slope, nrm, nin, hg, turned, b_out):
    images = token_pos.shape[1] // PATCH
    features, unit, quarter = nrm.shape[1], hg.shape[1], grads.shape[1]
    width = hid.shape[1]
    outs = (
        jax.ShapeDtypeStruct((width, quarter), BF16),
        jax.ShapeDtypeStruct((features, unit), F32),
        jax.ShapeDtypeStruct((40, 128), F32),
    )
    scratch = [
        pltpu.VMEM((images, WINDOW, quarter), BF16),
        pltpu.VMEM(hid.shape, BF16),
        pltpu.VMEM((images, PATCH + 8, unit), F32),
        pltpu.VMEM(slope.shape, F32),
        pltpu.VMEM(nin.shape, BF16),
        pltpu.VMEM(nrm.shape, BF16),
        pltpu.VMEM((width, quarter), F32),
        pltpu.VMEM((WINDOW, width), F32),
        pltpu.VMEM(slope.shape, BF16),
        DMA((4,)),
        DMA((images,)),
        DMA((images,)),
    ]
    specs = [SMEM] * 2 + [ANY] * 6 + [VMEM] * 2, [VMEM] * 3
    return call(product_kernel, outs, scratch, None, (counts, token_pos, grads, hid, slope, nrm, nin, hg, turned, b_out), 1 << 34, specs)


def last_kernel(
    wo, wi, vec, w_out, w_in, gain, bias, b_out, b_in, ry, ws, rx, ri, v1, t1, v2, t2, v3,
    y_s, y_r, x_s, x_r, i_s, i_r, a_s, a_r, b_s, b_r, d_s, d_r,
):
    layers, ny = v3.shape[0], wi.shape[0]
    z, xl, c = lax.axis_index("seq_0"), lax.axis_index("seq_1"), lax.axis_index("fsdp")
    y, xh = lax.axis_index("img_0"), lax.axis_index("img_1")

    def flip(me, bit):
        return 1 - me if bit else me

    plane = []
    for dy in range(ny):
        for dx in range(2):
            for dc in range(2):
                if (dy, dx, dc) != (0, 0, 0):
                    plane.append((dy, dx, dc))
    plane_ids = [((y + dy) % ny, flip(xh, dx), flip(c, dc)) for dy, dx, dc in plane]
    plane_dev = [{"img_0": a, "img_1": b, "fsdp": d} for a, b, d in plane_ids]
    side_dev = [{"seq_1": 1 - xl}, {"seq_1": 1 - xl, "img_1": 1 - xh}]
    corner = {"seq_1": 1 - xl, "fsdp": 1 - c}
    stack = [{"seq_0": (z + k) % layers} for k in range(1, layers)]
    greet(plane_dev + side_dev + [corner] + stack)
    ys = [{"img_0": (y + k) % ny} for k in range(1, ny)]
    started = []

    def go(copy):
        copy.start()
        started.append(copy)
        return copy

    stage_a = []
    for n, (dy, dx, dc) in enumerate(plane):
        if dc == 0:
            k = len(stage_a)
            stage_a.append(go(remote(vec, v1.at[k], a_s.at[k], a_r.at[k], plane_dev[n])))
    firsts = []
    for k in range(1, ny):
        firsts.append(go(remote(wo.at[:, (y + k) % ny], ry.at[k - 1], y_s.at[k - 1], y_r.at[k - 1], ys[k - 1])))
    ins = []
    for n, (dy, dx, dc) in enumerate(plane):
        a, b, d = plane_ids[n]
        ins.append((go(remote(wi.at[a, b, d], ri.at[n], i_s.at[n], i_r.at[n], plane_dev[n])), n, dc))
    total = vec[...]
    for k, copy in enumerate(stage_a):
        copy.wait_recv()
        total = total + v1[k]
    t1[...] = total
    q = xl * 2 + c
    stage_b = []
    for k, (dx, dc) in enumerate(((0, 1), (1, 0), (1, 1))):
        device = {"seq_1": flip(xl, dx), "fsdp": flip(c, dc)}
        stage_b.append(go(remote(t1, v2.at[q], b_s.at[k], b_r.at[k], device)))
    v2[q] = total
    for copy in stage_b:
        copy.wait_recv()
    t2[0:16] = v2[0, 0:16] + v2[1, 0:16] + v2[2, 0:16] + v2[3, 0:16]
    t2[16:32] = v2[0, 16:32] + v2[2, 16:32]
    t2[32:48] = v2[1, 16:32] + v2[3, 16:32]
    for j in range(4):
        t2[48 + j : 49 + j] = v2[j, 32:33]
    t2[52:56] = jnp.zeros((4, 128), F32)
    stage_d = []
    for k in range(1, layers):
        stage_d.append(go(remote(t2, v3.at[z], d_s.at[k - 1], d_r.at[k - 1], stack[k - 1])))
    v3[z] = t2[...]

    summed = wo[:, y].astype(F32)
    for k, copy in enumerate(firsts):
        copy.wait_recv()
        summed = summed + ry[k].astype(F32)
    block = ws.shape[2]
    for j in range(2):
        ws[:, j] = summed[:, j * block : (j + 1) * block].astype(BF16)
    outs = [
        (go(remote(ws.at[1 - xl, xh], rx.at[0], x_s.at[0], x_r.at[0], side_dev[0])), 0, 1),
        (go(remote(ws.at[1 - xl, 1 - xh], rx.at[1], x_s.at[1], x_r.at[1], side_dev[1])), 1, 1),
        (go(remote(ws.at[xl, 1 - xh], rx.at[2], x_s.at[2], x_r.at[2], {"img_1": 1 - xh})), 2, 0),
    ]

    same = wi[y, xh, c].astype(F32)
    cross = jnp.zeros_like(same)
    for copy, n, dc in ins:
        copy.wait_recv()
        if dc:
            cross = cross + ri[n].astype(F32)
        else:
            same = same + ri[n].astype(F32)
    width = same.shape[1]
    w_in[:, pl.ds(pl.multiple_of(c * width, 128), width)] = same
    w_in[:, pl.ds(pl.multiple_of((1 - c) * width, 128), width)] = cross
    near = ws[xl, xh].astype(F32)
    outs[2][0].wait_recv()
    near = near + rx[2].astype(F32)
    outs[0][0].wait_recv()
    outs[1][0].wait_recv()
    far = rx[0].astype(F32) + rx[1].astype(F32)
    width = near.shape[1]
    w_out[:, pl.ds(pl.multiple_of(xl * width, 128), width)] = near
    w_out[:, pl.ds(pl.multiple_of((1 - xl) * width, 128), width)] = far

    for copy in stage_d:
        copy.wait_recv()
    total = v3[0]
    for j in range(1, layers):
        total = total + v3[j]
    gain[...] = total[0:8]
    bias[...] = total[8:16]
    b_out[...] = total[16:48]
    for j in range(layers):
        b_in[4 * j : 4 * j + 4, :] = v3[j, 48:52]
    for copy in started:
        copy.wait_send()


def last(wo, wi, vec, layers):
    ny = wi.shape[0]
    members = ny * 4 - 1
    block = wi.shape[3:]
    outs = (
        jax.ShapeDtypeStruct((wo.shape[2] // 2, 2 * wo.shape[3]), F32),
        jax.ShapeDtypeStruct((block[0], 2 * block[1]), F32),
        jax.ShapeDtypeStruct((8, 128), F32),
        jax.ShapeDtypeStruct((8, 128), F32),
        jax.ShapeDtypeStruct((32, 128), F32),
        jax.ShapeDtypeStruct((4 * layers, 128), F32),
    )
    scratch = [
        pltpu.VMEM((ny - 1, 2, *wo.shape[2:]), BF16),
        pltpu.VMEM((2, 2, wo.shape[2] // 2, wo.shape[3]), BF16),
        pltpu.VMEM((3, wo.shape[2] // 2, wo.shape[3]), BF16),
        pltpu.VMEM((members, *block), F32),
        pltpu.VMEM((2 * ny - 1, 40, 128), F32),
        pltpu.VMEM((40, 128), F32),
        pltpu.VMEM((4, 40, 128), F32),
        pltpu.VMEM((56, 128), F32),
        pltpu.VMEM((layers, 56, 128), F32),
    ]
    for n in (ny - 1, 3, members, 2 * ny - 1, 3, layers - 1):
        scratch += [DMA((n,)), DMA((n,))]
    return call(last_kernel, outs, scratch, 1, (wo, wi, vec), 1 << 32)


def per_device(vision_feats, ln_gain, ln_bias, w_in, b_in, w_out, lm_grad, image_counts, token_pos):
    layers, ny = lax.axis_size("seq_0"), lax.axis_size("img_0")
    pieces = main(
        image_counts,
        token_pos,
        vision_feats[0],
        w_out,
        w_in,
        b_in.reshape(2, -1),
        lm_grad[0],
        ln_gain[None],
        ln_bias[None],
        layers,
    )
    w_out_part, w_in_part, vec = products(image_counts, token_pos, *pieces)
    quarter, unit = w_out_part.shape[1], w_in_part.shape[1]
    w_out_grad, w_in_grad, gain, bias, b_out, b_in_grad = last(
        w_out_part.reshape(2, ny, -1, quarter), w_in_part.reshape(ny, 2, 2, -1, unit), vec, layers
    )
    return (w_in_grad, b_in_grad.reshape(-1), w_out_grad, b_out.reshape(-1), gain.reshape(-1), bias.reshape(-1))


def solution(mesh):
    finer = Mesh(
        mesh.devices.reshape(8, 2, 4, 2, mesh.shape["fsdp"]),
        ("seq_0", "seq_1", "img_0", "img_1", "fsdp"),
    )
    placed = (
        P(IMG, SEQ_FSDP, None),
        P(),
        P(),
        P("fsdp", SEQ),
        P(SEQ),
        P(SEQ, "fsdp"),
        P(IMG, SEQ, "fsdp"),
        P(IMG, None),
        P(IMG, None),
    )
    return jax.shard_map(
        per_device,
        mesh=finer,
        in_specs=placed,
        out_specs=(P(IMG_FSDP, SEQ), P(), P(SEQ_IMG, "fsdp"), P(), P(), P()),
        check_vma=False,
    )
```

time: 237 us -> 184 us (0.78)
  Pallas kernels: 117 us -> 174 us
  local copies, waits for them, and re-layouts: 51.9 us -> 8.33 us
  matrix products: 26.8 us -> 0 us
  other arithmetic: 22.7 us -> 0 us
  between operations: 17.2 us -> 0.66 us
    pallas_call x4 -> x3, Pallas kernels: 117 us -> 174 us  [call(): pl.pallas_call(kernel, out_shape=tuple(outs), in_specs=ins, out_specs=tup...]
    dot_general x8 -> x0, matrix products: 26.8 us -> none  [the longest x7 26.5 us: contract(): lax.dot_general(left, right, (((left_dim,), (right_dim,)), ((), ())), pre...]
    dynamic_update_slice x5 -> x0, local copies, waits for them, and re-layouts: 15.8 us -> none  [the longest x4 15.6 us: per_device(): lax.dynamic_update_slice(hidden_pos, hidden[i * PATCH:(i + 1) * PATCH], (...]
    convert_element_type x2 -> x0, other arithmetic: 9.83 us -> none  [the longest x1 6.26 us: per_device(): normed = normed.astype(BF16).reshape(rows, -1)]
    reduce_sum x4 -> x0, other arithmetic: 8.53 us -> none  [the longest x1 3.83 us: per_device(): row_var = jnp.mean(centred * centred, axis=-1, keepdims=True)]
    dot_general x1 -> x0, local copies, waits for them, and re-layouts: 6.8 us -> none  [contract(): lax.dot_general(left, right, (((left_dim,), (right_dim,)), ((), ())), pre...]
    dynamic_slice x4 -> x0, local copies, waits for them, and re-layouts: 6.27 us -> none  [the longest x1 4.78 us: per_device(): lax.dynamic_index_in_dim(hidden_pos, 1 - xl, 1, keepdims=False)]
    unnamed x40 -> x6, local copies, waits for them, and re-layouts: 13.5 us -> 8.33 us
  transfers between devices with their start and end apart: 2 -> 0, of which waited for: 0 -> 0; matrix products, arithmetic and copies ran while one was open for 29% -> 0% of each run, Pallas kernels for 24% -> 0%
where the time goes in v2:
time: 184 us; the launch traced here: 183 us
  Pallas kernels  174 us (95%)
  local copies, waits for them, and re-layouts  8.33 us (5%)
    pallas_call x3, Pallas kernels, call(): pl.pallas_call(kernel, out_shape=tuple(outs), in_specs=ins, out_specs=tup...  174 us
    unnamed x6, local copies, waits for them, and re-layouts  8.33 us

profile of v2, /device:TPU:1, one launch (start us, length us, event | category | flops | bytes accessed | tf_op | source)
XLA Modules:
  0.0 182.8 jit_solution(6719772058512641525)
XLA Ops:
  0.6 130.6 %shard_map.136 = (bf16[4096,1024]{1,0:T(8,128)(2,1)}, bf16[2304,512]{1,0:T(8,128)(2,1)}, f32[2304,128]{1,0:T(8,128)}, bf16[2304,1024]{1,0:T(8,128)(2,1)}, bf16[2...) custom-call(s32[1,2]{1,0:T(1,128)} %counts.3, s32[1,2304]{1,0:T(1,128)} %token_pos.3, ...), custom_call_target="tpu_custom_call" | custom-call | flops 17179869184 | bytes 1048576 | tf_op jit(solution)/shard_map/pallas_call | solution.py:42
  131.2 13.1 %shard_map.137 = (bf16[512,1024]{1,0:T(8,128)(2,1)}, f32[1024,128]{1,0:T(8,128)}, f32[40,128]{1,0:T(8,128)}) custom-call(s32[1,2]{1,0:T(1,128)} %counts.3, s32[1,2304]{1,0:T(1,128)} %token_pos.3, bf16[4096,1024]{1,0:T(8,128)(2,1)} %get-tuple-element.23.grads, bf16[2304,512]{1,0:T(8,128)(2,1)} %get-tuple-element.24.hid, f32[2304,128]{1,0:T(8,128)} %get-tuple-element.25.slope, ...), custom_call_target="tpu_custom_call" | custom-call | flops 17179869184 | bytes 1048576 | tf_op jit(solution)/shard_map/pallas_call | solution.py:42
  144.4 30.1 %shard_map.138 = (f32[32,2048]{1,0:T(8,128)}, f32[64,256]{1,0:T(8,128)}, f32[8,128]{1,0:T(8,128)}, f32[8,128]{1,0:T(8,128)}, f32[32,128]{1,0:T(8,128)}, /*index=5*/f32[32,128]{1,0:T(8,128)}) custom-call(bf16[2,4,64,1024]{3,2,1,0:T(8,128)(2,1)} %bitcast.20, f32[4,2,2,64,128]{4,3,2,1,0:T(8,128)} %bitcast.21, f32[40,128]{1,0:T(8,128)} %get-tuple-element.33.vec), custom_call_target="tpu_custom_call" | custom-call | flops 4294967296 | bytes 1048576 | tf_op jit(solution)/shard_map/pallas_call | solution.py:42
  174.4 1.5 copy.21
  175.9 1.3 copy.22
  177.2 1.7 copy.23
  178.9 1.3 copy.24
  180.2 1.3 copy.25
  181.5 1.3 copy.26

commit v3 on v2

--- a/solution.py
+++ b/solution.py
@@ -22,6 +22,7 @@
 DMA = pltpu.SemaphoreType.DMA
 LIMIT = 63 * 1024 * 1024
 WINDOW = 640
+SUB = 2
 
 
 def remote(src, dst, send, recv, device):
@@ -30,11 +31,15 @@
     )
 
 
-def greet(devices):
+def signal(devices):
     barrier = pltpu.get_barrier_semaphore()
     for device in devices:
         pl.semaphore_signal(barrier, inc=1, device_id=device, device_id_type=MESH)
-    pl.semaphore_wait(barrier, len(devices))
+
+
+def greet(devices):
+    signal(devices)
+    pl.semaphore_wait(pltpu.get_barrier_semaphore(), len(devices))
 
 
 def call(kernel, outs, scratch, number, args, flops, specs=None):
@@ -70,7 +75,7 @@
 def main_kernel(
     counts, token_pos, v, wo, wi, bi, lm, gain, bias,
     grads_out, hid_out, slope_out, nrm_out, nin_out, hg_out, turned, b_out,
-    grads, vs, wq, wis, bis, mine, r1, give, r2, hg, nrm, nin, hid, slope, pre, nf,
+    grads, vs, wq, wis, bis, mine, r1, give, r2, hg, nrm, nin, hid, slope, pre, nf, held,
     vu_s, vu_r, vd_s, vd_r, vx_s, vx_r, vc_s, vc_r,
     pu_s, pu_r, pd_s, pd_r, px_s, px_r, wx_s, wx_r, wc_s, wc_r,
     h1_s, h1_r, h2_s, h2_r, local, put_p, put_v, put_h,
@@ -98,13 +103,14 @@
     def rows(zb, xq, k):
         return pl.ds(pl.multiple_of((zb * 2 + xq) * block_rows + k * chunk, 128), chunk)
 
-    def ring_p(s, t, upward):
+    def ring_p(s, t, upward, u):
         xq = xl if t == 0 else other
+        size = chunk // SUB
+        zb, k = (below(s), 0) if upward else (above(s), 1)
+        r = pl.ds(pl.multiple_of((zb * 2 + xq) * block_rows + k * chunk + u * size, 16), size)
         if upward:
-            r = rows(below(s), xq, 0)
-            return lambda n: remote(grads.at[r], grads.at[r], pu_s.at[n, t], pu_r.at[n, t], up)
-        r = rows(above(s), xq, 1)
-        return lambda n: remote(grads.at[r], grads.at[r], pd_s.at[n, t], pd_r.at[n, t], down)
+            return lambda n: remote(grads.at[r], grads.at[r], pu_s.at[n, t, u], pu_r.at[n, t, u], up)
+        return lambda n: remote(grads.at[r], grads.at[r], pd_s.at[n, t, u], pd_r.at[n, t, u], down)
 
     def ring_v(s, upward):
         zb = below(s) if upward else above(s)
@@ -121,10 +127,11 @@
         ref = vs.at[below(s) if d == 0 else above(s), xq, cq]
         return remote(ref, ref, vc_s.at[t, d, s], vc_r.at[t, d, s], twin)
 
-    def p_swap(k, xq):
-        r = rows(z, xq, k)
-        source = lm.at[pl.ds(k * chunk, chunk), their_cols]
-        return remote(source, grads.at[r], px_s.at[k], px_r.at[k], across)
+    def p_swap(u, k, xq):
+        size = chunk // SUB
+        r = pl.ds(pl.multiple_of((z * 2 + xq) * block_rows + k * chunk + u * size, 16), size)
+        source = lm.at[pl.ds(k * chunk + u * size, size), their_cols]
+        return remote(source, grads.at[r], px_s.at[u, k], px_r.at[u, k], across)
 
     def w_in_at(cq, xq):
         size = wi.shape[0]
@@ -151,65 +158,69 @@
     def h_across(s):
         return remote(give.at[s], r2.at[s], h2_s.at[s], h2_r.at[s], across)
 
-    greet([up, down, across, twin])
+    signal([up, down, across, twin])
     locals_ = [
+        pltpu.make_async_copy(v, vs.at[z, xl, c], local.at[2]),
         pltpu.make_async_copy(lm.at[pl.ds(0, chunk), mine_cols], grads.at[rows(z, xl, 0)], local.at[0]),
         pltpu.make_async_copy(lm.at[pl.ds(chunk, chunk), mine_cols], grads.at[rows(z, xl, 1)], local.at[1]),
-        pltpu.make_async_copy(v, vs.at[z, xl, c], local.at[2]),
+        pltpu.make_async_copy(wi, w_in_at(c, xl), local.at[4]),
         pltpu.make_async_copy(wo.at[:, mine_cols], w_out_at(xl), local.at[3]),
-        pltpu.make_async_copy(wi, w_in_at(c, xl), local.at[4]),
         pltpu.make_async_copy(bi, bis.at[xl], local.at[5]),
+        pltpu.make_async_copy(lm, held, local.at[6]),
     ]
     for copy in locals_:
         copy.start()
-    p_swap(0, xl).start()
-    p_swap(1, xl).start()
-    for n in range(3):
-        w_swap(n, xl).start()
-    locals_[2].wait()
+    pl.semaphore_wait(pltpu.get_barrier_semaphore(), 4)
+    for u in range(SUB):
+        for k in range(2):
+            p_swap(u, k, xl).start()
+    locals_[0].wait()
     ring_v(0, True)(0).start()
     ring_v(0, False)(0).start()
-    for copy in locals_[:2]:
+    for copy in locals_[1:3]:
         copy.wait()
-    ring_p(0, 0, True)(0).start()
-    ring_p(0, 0, False)(0).start()
+    for u in range(SUB):
+        ring_p(0, 0, True, u)(0).start()
+        ring_p(0, 0, False, u)(0).start()
     v_across(0, 0, xl).start()
+    for n in (1, 2, 0):
+        w_swap(n, xl).start()
     v_twin(0, 0, xl, 0, c).start()
-    for copy in locals_[3:]:
+    for copy in locals_[3:6]:
         copy.wait()
     w_twin(0, c).start()
 
+    def put_chunk(s, t, upward):
+        r = rows(below(s) if upward else above(s), xl if t == 0 else other, 0 if upward else 1)
+        return pltpu.make_async_copy(grads.at[r], grads_out.at[r], put_p.at[s, t, 0 if upward else 1])
+
+    def put_layer(s, d, n):
+        r = pl.ds(pl.multiple_of((below(s) if d == 0 else above(s)) * layer_rows, 32), layer_rows)
+        source = (hid, slope, nrm, nin)[n]
+        target = (hid_out, slope_out, nrm_out, nin_out)[n]
+        return pltpu.make_async_copy(source.at[r], target.at[r], put_v.at[s, d, n])
+
+    def put_sum(s, xq, k):
+        r = rows(below(s) if k == 0 else above(s), xq, k)
+        return pltpu.make_async_copy(hg.at[r], hg_out.at[r], put_h.at[s, xq, k])
+
+    for u in range(SUB):
+        p_swap(u, 0, other).wait_recv()
+        ring_p(0, 1, True, u)(0).start()
+        p_swap(u, 1, other).wait_recv()
+        ring_p(0, 1, False, u)(0).start()
+    for t in range(2):
+        put_chunk(0, t, True).start()
+        put_chunk(0, t, False).start()
+    locals_[6].wait()
     starts = image_starts(counts, token_pos)
     here = (z * 2 + xl) * block_rows + lax.broadcasted_iota(jnp.int32, (block_rows, 1), 0)
     taken = jnp.zeros((block_rows, 1), F32)
     for start in starts:
         taken = taken + jnp.where((here >= start) & (here < start + PATCH), 1.0, 0.0)
     for j in range(lm.shape[1] // 128):
-        column = lm[:, j * 128 : (j + 1) * 128].astype(F32) * taken
+        column = held[:, j * 128 : (j + 1) * 128].astype(F32) * taken
         b_out[j : j + 1, :] = jnp.sum(column, axis=0, keepdims=True)
-    def put_chunk(s, t, upward):
-        r = rows(below(s) if upward else above(s), xl if t == 0 else other, 0 if upward else 1)
-        return pltpu.make_async_copy(grads.at[r], grads_out.at[r], put_p.at[s, t, 0 if upward else 1])
-
-    def put_layer(s, d, n):
-        r = pl.ds(pl.multiple_of((below(s) if d == 0 else above(s)) * layer_rows, 32), layer_rows)
-        source = (hid, slope, nrm, nin)[n]
-        target = (hid_out, slope_out, nrm_out, nin_out)[n]
-        return pltpu.make_async_copy(source.at[r], target.at[r], put_v.at[s, d, n])
-
-    def put_sum(s, xq, k):
-        r = rows(below(s) if k == 0 else above(s), xq, k)
-        return pltpu.make_async_copy(hg.at[r], hg_out.at[r], put_h.at[s, xq, k])
-
-    put_chunk(0, 0, True).start()
-    put_chunk(0, 0, False).start()
-    p_swap(0, other).wait_recv()
-    ring_p(0, 1, True)(0).start()
-    put_chunk(0, 1, True).start()
-    p_swap(1, other).wait_recv()
-    ring_p(0, 1, False)(0).start()
-    put_chunk(0, 1, False).start()
-
     def multiply(s):
         for xq in range(2):
             for k in range(2):
@@ -289,24 +300,26 @@
             v_across(s, 1, xl).start()
             v_twin(s, 1, xl, 0, c).start()
 
-        @pl.when(s - 1 <= v_up)
-        def _():
-            v_across(s - 1, 0, other).wait_recv()
-            v_twin(s - 1, 0, other, 1, c).start()
-
-        @pl.when((s >= 2) & (s - 1 <= v_down))
-        def _():
-            v_across(s - 1, 1, other).wait_recv()
-            v_twin(s - 1, 1, other, 1, c).start()
+        @pl.when((s >= 2) & (s - 2 <= v_up))
+        def _():
+            v_across(s - 2, 0, other).wait_recv()
+            v_twin(s - 2, 0, other, 1, c).start()
+
+        @pl.when((s >= 3) & (s - 2 <= v_down))
+        def _():
+            v_across(s - 2, 1, other).wait_recv()
+            v_twin(s - 2, 1, other, 1, c).start()
 
     def serve_p(s, t):
+        for u in range(SUB):
+            for upward in (True, False):
+                ring_p(s, t, upward, u)(s - 1).wait_recv()
+
+                @pl.when(s < layers - 1)
+                def _():
+                    ring_p(s, t, upward, u)(s).start()
+
         for upward in (True, False):
-            ring_p(s, t, upward)(s - 1).wait_recv()
-
-            @pl.when(s < layers - 1)
-            def _():
-                ring_p(s, t, upward)(s).start()
-
             put_chunk(s, t, upward).start()
 
     def use_v(s):
@@ -327,18 +340,18 @@
                 put_layer(s, 1, n).start()
 
     def count(s):
-        return jnp.maximum(jnp.minimum(2 * s - 3, s), 0)
+        return jnp.maximum(jnp.minimum(2 * s - 4, s), 0)
 
     def step(s, carry):
         serve_v(s)
         serve_p(s, 0)
 
-        @pl.when(s == 1)
+        @pl.when(s == 2)
         def _():
             w_swap(1, other).wait_recv()
             w_twin(1, c).start()
 
-        @pl.when(s == 2)
+        @pl.when(s == 3)
         def _():
             w_swap(0, other).wait_recv()
             w_swap(2, other).wait_recv()
@@ -362,8 +375,9 @@
     span(add_twin, layers - 2, layers)
     span(add_across, layers - 3, layers)
 
-    for k in range(2):
-        p_swap(k, xl).wait_send()
+    for u in range(SUB):
+        for k in range(2):
+            p_swap(u, k, xl).wait_send()
     for n in range(3):
         w_swap(n, xl).wait_send()
     for t in range(2):
@@ -372,7 +386,8 @@
     def sent_p(s, carry):
         for t in range(2):
             for upward in (True, False):
-                ring_p(s, t, upward)(s).wait_send()
+                for u in range(SUB):
+                    ring_p(s, t, upward, u)(s).wait_send()
         return carry
 
     lax.fori_loop(0, layers - 1, sent_p, 0)
@@ -443,14 +458,15 @@
         pltpu.VMEM((tokens, unit), F32),
         pltpu.VMEM((layer_rows, hid), F32),
         pltpu.VMEM((layer_rows, features), F32),
+        pltpu.VMEM((rows, width), BF16),
     ]
     half = layers // 2
-    sems = [(half,), (half - 1,), (2, half + 1), (2, 2, half + 1), (layers - 1, 2), (layers - 1, 2), (2,), (3,), (2,)]
+    sems = [(half,), (half - 1,), (2, half + 1), (2, 2, half + 1), (layers - 1, 2, SUB), (layers - 1, 2, SUB), (SUB, 2), (3,), (2,)]
     sems += [(layers, 2), (layers,)]
     for shape in sems:
         scratch += [DMA(shape), DMA(shape)]
-    scratch += [DMA((6,)), DMA((layers, 2, 2)), DMA((half + 1, 2, 4)), DMA((layers, 2, 2))]
-    specs = [SMEM] * 2 + [VMEM] * 7, [ANY] * 6 + [VMEM] * 2
+    scratch += [DMA((7,)), DMA((layers, 2, 2)), DMA((half + 1, 2, 4)), DMA((layers, 2, 2))]
+    specs = [SMEM] * 2 + [ANY] * 5 + [VMEM] * 2, [ANY] * 6 + [VMEM] * 2
     return call(main_kernel, outs, scratch, 0, (counts, token_pos, v, wo, wi, bi, lm, gain, bias), 1 << 34, specs)
 
 
@@ -499,7 +515,7 @@
         total = total + jnp.sum(pg.astype(F32), axis=0, keepdims=True)
     vec[32:33, :] = total
     others[2].wait()
-    w_in_part[...] = contract(pgs[...], rv[...], 0, 0).T
+    w_in_part[...] = contract(pgs[...], rv[...], 0, 0).T.astype(BF16)
     others[3].wait()
     moment = contract(pgs[...], nv[...], 0, 0)
     column = contract(pgs[...], jnp.ones((pgs.shape[0], 128), BF16), 0, 0)
@@ -515,7 +531,7 @@
     width = hid.shape[1]
     outs = (
         jax.ShapeDtypeStruct((width, quarter), BF16),
-        jax.ShapeDtypeStruct((features, unit), F32),
+        jax.ShapeDtypeStruct((features, unit), BF16),
         jax.ShapeDtypeStruct((40, 128), F32),
     )
     scratch = [
@@ -537,8 +553,9 @@
 
 
 def last_kernel(
-    wo, wi, vec, w_out, w_in, gain, bias, b_out, b_in, ry, ws, rx, ri, v1, t1, v2, t2, v3,
-    y_s, y_r, x_s, x_r, i_s, i_r, a_s, a_r, b_s, b_r, d_s, d_r,
+    wo, wi, vec, w_out, w_in, gain, bias, b_out, b_in,
+    ry1, s1, rx1, rx2, s2, ry2, ri, v1, t1, v2, t2, v3,
+    y1_s, y1_r, x1_s, x1_r, x2_s, x2_r, y2_s, y2_r, i_s, i_r, a_s, a_r, b_s, b_r, d_s, d_r,
 ):
     layers, ny = v3.shape[0], wi.shape[0]
     z, xl, c = lax.axis_index("seq_0"), lax.axis_index("seq_1"), lax.axis_index("fsdp")
@@ -572,9 +589,16 @@
         if dc == 0:
             k = len(stage_a)
             stage_a.append(go(remote(vec, v1.at[k], a_s.at[k], a_r.at[k], plane_dev[n])))
-    firsts = []
-    for k in range(1, ny):
-        firsts.append(go(remote(wo.at[:, (y + k) % ny], ry.at[k - 1], y_s.at[k - 1], y_r.at[k - 1], ys[k - 1])))
+    half = ry1.shape[4]
+    left, right = pl.ds(0, half), pl.ds(half, half)
+    across = [(1 - xl, xh), (1 - xl, 1 - xh), (xl, 1 - xh)]
+    across_dev = side_dev + [{"img_1": 1 - xh}]
+    x_first, y_first = [], []
+    for m, (p, h) in enumerate(across):
+        x_first.append(go(remote(wo.at[p, :, h, :, right], rx2.at[m], x2_s.at[m], x2_r.at[m], across_dev[m])))
+    for k in range(ny - 1):
+        source = wo.at[:, (y + k + 1) % ny, :, :, left]
+        y_first.append(go(remote(source, ry1.at[k], y1_s.at[k], y1_r.at[k], ys[k])))
     ins = []
     for n, (dy, dx, dc) in enumerate(plane):
         a, b, d = plane_ids[n]
@@ -590,6 +614,23 @@
         device = {"seq_1": flip(xl, dx), "fsdp": flip(c, dc)}
         stage_b.append(go(remote(t1, v2.at[q], b_s.at[k], b_r.at[k], device)))
     v2[q] = total
+    summed = wo[:, y, :, :, 0:half].astype(F32)
+    for k, copy in enumerate(y_first):
+        copy.wait_recv()
+        summed = summed + ry1[k].astype(F32)
+    s1[...] = summed.astype(BF16)
+    x_second = []
+    for m, (p, h) in enumerate(across):
+        x_second.append(go(remote(s1.at[p, h], rx1.at[m], x1_s.at[m], x1_r.at[m], across_dev[m])))
+    for copy in x_first:
+        copy.wait_recv()
+    s2[0] = (wo[xl, :, xh, :, half:].astype(F32) + rx2[2].astype(F32)).astype(BF16)
+    s2[1] = (rx2[0].astype(F32) + rx2[1].astype(F32)).astype(BF16)
+    y_second = []
+    for k in range(ny - 1):
+        y_second.append(
+            go(remote(s2.at[:, (y + k + 1) % ny], ry2.at[k], y2_s.at[k], y2_r.at[k], ys[k]))
+        )
     for copy in stage_b:
         copy.wait_recv()
     t2[0:16] = v2[0, 0:16] + v2[1, 0:16] + v2[2, 0:16] + v2[3, 0:16]
@@ -603,19 +644,6 @@
         stage_d.append(go(remote(t2, v3.at[z], d_s.at[k - 1], d_r.at[k - 1], stack[k - 1])))
     v3[z] = t2[...]
 
-    summed = wo[:, y].astype(F32)
-    for k, copy in enumerate(firsts):
-        copy.wait_recv()
-        summed = summed + ry[k].astype(F32)
-    block = ws.shape[2]
-    for j in range(2):
-        ws[:, j] = summed[:, j * block : (j + 1) * block].astype(BF16)
-    outs = [
-        (go(remote(ws.at[1 - xl, xh], rx.at[0], x_s.at[0], x_r.at[0], side_dev[0])), 0, 1),
-        (go(remote(ws.at[1 - xl, 1 - xh], rx.at[1], x_s.at[1], x_r.at[1], side_dev[1])), 1, 1),
-        (go(remote(ws.at[xl, 1 - xh], rx.at[2], x_s.at[2], x_r.at[2], {"img_1": 1 - xh})), 2, 0),
-    ]
-
     same = wi[y, xh, c].astype(F32)
     cross = jnp.zeros_like(same)
     for copy, n, dc in ins:
@@ -627,15 +655,21 @@
     width = same.shape[1]
     w_in[:, pl.ds(pl.multiple_of(c * width, 128), width)] = same
     w_in[:, pl.ds(pl.multiple_of((1 - c) * width, 128), width)] = cross
-    near = ws[xl, xh].astype(F32)
-    outs[2][0].wait_recv()
-    near = near + rx[2].astype(F32)
-    outs[0][0].wait_recv()
-    outs[1][0].wait_recv()
-    far = rx[0].astype(F32) + rx[1].astype(F32)
-    width = near.shape[1]
-    w_out[:, pl.ds(pl.multiple_of(xl * width, 128), width)] = near
-    w_out[:, pl.ds(pl.multiple_of((1 - xl) * width, 128), width)] = far
+    for copy in x_second:
+        copy.wait_recv()
+    near = s1[xl, xh].astype(F32) + rx1[2].astype(F32)
+    far = rx1[0].astype(F32) + rx1[1].astype(F32)
+    near_at = pl.multiple_of(2 * half * xl, 128)
+    far_at = pl.multiple_of(2 * half * (1 - xl), 128)
+    w_out[:, pl.ds(near_at, half)] = near
+    w_out[:, pl.ds(far_at, half)] = far
+    near, far = s2[0, y].astype(F32), s2[1, y].astype(F32)
+    for k, copy in enumerate(y_second):
+        copy.wait_recv()
+        near = near + ry2[k, 0].astype(F32)
+        far = far + ry2[k, 1].astype(F32)
+    w_out[:, pl.ds(near_at + half, half)] = near
+    w_out[:, pl.ds(far_at + half, half)] = far
 
     for copy in stage_d:
         copy.wait_recv()
@@ -655,8 +689,9 @@
     ny = wi.shape[0]
     members = ny * 4 - 1
     block = wi.shape[3:]
+    rows, half = wo.shape[3], wo.shape[4] // 2
     outs = (
-        jax.ShapeDtypeStruct((wo.shape[2] // 2, 2 * wo.shape[3]), F32),
+        jax.ShapeDtypeStruct((rows, 4 * half), F32),
         jax.ShapeDtypeStruct((block[0], 2 * block[1]), F32),
         jax.ShapeDtypeStruct((8, 128), F32),
         jax.ShapeDtypeStruct((8, 128), F32),
@@ -664,19 +699,33 @@
         jax.ShapeDtypeStruct((4 * layers, 128), F32),
     )
     scratch = [
-        pltpu.VMEM((ny - 1, 2, *wo.shape[2:]), BF16),
-        pltpu.VMEM((2, 2, wo.shape[2] // 2, wo.shape[3]), BF16),
-        pltpu.VMEM((3, wo.shape[2] // 2, wo.shape[3]), BF16),
-        pltpu.VMEM((members, *block), F32),
+        pltpu.VMEM((ny - 1, 2, 2, rows, half), BF16),
+        pltpu.VMEM((2, 2, rows, half), BF16),
+        pltpu.VMEM((3, rows, half), BF16),
+        pltpu.VMEM((3, ny, rows, half), BF16),
+        pltpu.VMEM((2, ny, rows, half), BF16),
+        pltpu.VMEM((ny - 1, 2, rows, half), BF16),
+        pltpu.VMEM((members, *block), BF16),
         pltpu.VMEM((2 * ny - 1, 40, 128), F32),
         pltpu.VMEM((40, 128), F32),
         pltpu.VMEM((4, 40, 128), F32),
         pltpu.VMEM((56, 128), F32),
         pltpu.VMEM((layers, 56, 128), F32),
     ]
-    for n in (ny - 1, 3, members, 2 * ny - 1, 3, layers - 1):
+    for n in (ny - 1, 3, 3, ny - 1, members, 2 * ny - 1, 3, layers - 1):
         scratch += [DMA((n,)), DMA((n,))]
     return call(last_kernel, outs, scratch, 1, (wo, wi, vec), 1 << 32)
+
+
+def copy_kernel(*refs):
+    count = len(refs) // 2
+    for source, target in zip(refs[:count], refs[count:]):
+        target[...] = source[...]
+
+
+def result_of(arrays):
+    outs = [jax.ShapeDtypeStruct(a.shape, a.dtype) for a in arrays]
+    return call(copy_kernel, outs, [], None, arrays, 1 << 20)
 
 
 def per_device(vision_feats, ln_gain, ln_bias, w_in, b_in, w_out, lm_grad, image_counts, token_pos):
@@ -695,9 +744,8 @@
     )
     w_out_part, w_in_part, vec = products(image_counts, token_pos, *pieces)
     quarter, unit = w_out_part.shape[1], w_in_part.shape[1]
-    w_out_grad, w_in_grad, gain, bias, b_out, b_in_grad = last(
-        w_out_part.reshape(2, ny, -1, quarter), w_in_part.reshape(ny, 2, 2, -1, unit), vec, layers
-    )
+    sums = last(w_out_part.reshape(2, ny, 2, -1, quarter), w_in_part.reshape(ny, 2, 2, -1, unit), vec, layers)
+    w_out_grad, w_in_grad, gain, bias, b_out, b_in_grad = result_of(sums)
     return (w_in_grad, b_in_grad.reshape(-1), w_out_grad, b_out.reshape(-1), gain.reshape(-1), bias.reshape(-1))
 
 

time: 184 us -> 161 us (0.88)
  Pallas kernels: 174 us -> 160 us
  local copies, waits for them, and re-layouts: 8.33 us -> 0 us
    pallas_call x3 -> x4, Pallas kernels: 174 us -> 160 us  [call(): pl.pallas_call(kernel, out_shape=tuple(outs), in_specs=ins, out_specs=tup...]
    unnamed x6 -> x0, local copies, waits for them, and re-layouts: 8.33 us -> none
where the time goes in v3:
time: 161 us
  Pallas kernels  160 us (99%)
    pallas_call x4, Pallas kernels, call(): pl.pallas_call(kernel, out_shape=tuple(outs), in_specs=ins, out_specs=tup...  160 us

profile of v3, /device:TPU:1, one launch (start us, length us, event | category | flops | bytes accessed | tf_op | source)
XLA Modules:
  0.0 161.1 jit_solution(10105503762750307105)
XLA Ops:
  0.6 115.6 %shard_map.136 = (bf16[4096,1024]{1,0:T(8,128)(2,1)}, bf16[2304,512]{1,0:T(8,128)(2,1)}, f32[2304,128]{1,0:T(8,128)}, bf16[2304,1024]{1,0:T(8,128)(2,1)}, bf16[2...) custom-call(s32[1,2]{1,0:T(1,128)} %counts.3, s32[1,2304]{1,0:T(1,128)} %token_pos.3, ...), custom_call_target="tpu_custom_call" | custom-call | flops 17179869184 | bytes 1048576 | tf_op jit(solution)/shard_map/pallas_call | solution.py:47
  116.2 13.1 %shard_map.137 = (bf16[512,1024]{1,0:T(8,128)(2,1)}, bf16[1024,128]{1,0:T(8,128)(2,1)}, f32[40,128]{1,0:T(8,128)}) custom-call(s32[1,2]{1,0:T(1,128)} %counts.3, s32[1,2304]{1,0:T(1,128)} %token_pos.3, bf16[4096,1024]{1,0:T(8,128)(2,1)} %get-tuple-element.29.grads, bf16[2304,512]{1,0:T(8,128)(2,1)} %get-tuple-element.30.hid, ...), custom_call_target="tpu_custom_call" | custom-call | flops 17179869184 | bytes 1048576 | tf_op jit(solution)/shard_map/pallas_call | solution.py:47
  129.4 30.0 %shard_map.138 = (f32[32,2048]{1,0:T(8,128)}, f32[64,256]{1,0:T(8,128)}, f32[8,128]{1,0:T(8,128)}, f32[8,128]{1,0:T(8,128)}, f32[32,128]{1,0:T(8,128)}, /*index=5*/f32[32,128]{1,0:T(8,128)}) custom-call(bf16[2,4,2,32,1024]{4,3,2,1,0:T(8,128)(2,1)} %bitcast.20, bf16[4,2,2,64,128]{4,3,2,1,0:T(8,128)(2,1)} %bitcast.21, f32[40,128]{1,0:T(8,128)} %get-tuple-element.39.vec), custom_call_target="tpu_custom_call" | custom-call | flops 4294967296 | bytes 1048576 | tf_op jit(solution)/shard_map/pallas_call | solution.py:47
  159.4 1.7 %shard_map.139 = (f32[32,2048]{1,0:T(8,128)}, f32[64,256]{1,0:T(8,128)}, f32[8,128]{1,0:T(8,128)}, f32[8,128]{1,0:T(8,128)}, f32[32,128]{1,0:T(8,128)}, /*index=5*/f32[32,128]{1,0:T(8,128)}) custom-call(f32[32,2048]{1,0:T(8,128)} %get-tuple-element.40.refs_0_, f32[64,256]{1,0:T(8,128)} %get-tuple-element.41.refs_1_, f32[8,128]{1,0:T(8,128)} %get-tuple-element.42.refs_2_, ...), custom_call_target="tpu_custom_call" | custom-call | flops 1048576 | bytes 1048576 | tf_op jit(solution)/shard_map/pallas_call | solution.py:47

commit v4 on v3

--- a/solution.py
+++ b/solution.py
@@ -76,7 +76,7 @@
     counts, token_pos, v, wo, wi, bi, lm, gain, bias,
     grads_out, hid_out, slope_out, nrm_out, nin_out, hg_out, turned, b_out,
     grads, vs, wq, wis, bis, mine, r1, give, r2, hg, nrm, nin, hid, slope, pre, nf, held,
-    vu_s, vu_r, vd_s, vd_r, vx_s, vx_r, vc_s, vc_r,
+    vu_s, vu_r, vd_s, vd_r, vh_s, vh_r, vx_s, vx_r, vc_s, vc_r,
     pu_s, pu_r, pd_s, pd_r, px_s, px_r, wx_s, wx_r, wc_s, wc_r,
     h1_s, h1_r, h2_s, h2_r, local, put_p, put_v, put_h,
 ):
@@ -277,28 +277,38 @@
 
     v_up, v_down = layers // 2, layers // 2 - 1
 
+    def half_v(s, upward):
+        size = vs.shape[4] // 2
+        if upward:
+            ref = vs.at[below(s), xl, c, :, pl.ds(0, size)]
+            return remote(ref, ref, vh_s.at[0], vh_r.at[0], up)
+        ref = vs.at[above(s), xl, c, :, pl.ds(size, size)]
+        return remote(ref, ref, vh_s.at[1], vh_r.at[1], down)
+
     def serve_v(s):
-        @pl.when(s <= v_up)
+        for d, upward in enumerate((True, False)):
+
+            @pl.when(s <= v_down)
+            def _():
+                ring_v(s, upward)(s - 1).wait_recv()
+
+                @pl.when(s < v_down)
+                def _():
+                    ring_v(s, upward)(s).start()
+
+                @pl.when(s == v_down)
+                def _():
+                    half_v(s, upward).start()
+
+                v_across(s, d, xl).start()
+                v_twin(s, d, xl, 0, c).start()
+
+        @pl.when(s == v_up)
         def _():
-            ring_v(s, True)(s - 1).wait_recv()
-
-            @pl.when(s < v_up)
-            def _():
-                ring_v(s, True)(s).start()
-
+            half_v(s, True).wait_recv()
+            half_v(s, False).wait_recv()
             v_across(s, 0, xl).start()
             v_twin(s, 0, xl, 0, c).start()
-
-        @pl.when(s <= v_down)
-        def _():
-            ring_v(s, False)(s - 1).wait_recv()
-
-            @pl.when(s < v_down)
-            def _():
-                ring_v(s, False)(s).start()
-
-            v_across(s, 1, xl).start()
-            v_twin(s, 1, xl, 0, c).start()
 
         @pl.when((s >= 2) & (s - 2 <= v_up))
         def _():
@@ -406,10 +416,10 @@
         h_across(s).wait_send()
 
     span(sent_h, 0, layers)
-    for s in range(v_up):
-        ring_v(s, True)(s).wait_send()
-    for s in range(v_down):
-        ring_v(s, False)(s).wait_send()
+    for upward in (True, False):
+        for s in range(v_down):
+            ring_v(s, upward)(s).wait_send()
+        half_v(v_down, upward).wait_send()
     for s in range(v_up + 1):
         for d in range(2):
             if d == 0 or 1 <= s <= v_down:
@@ -461,7 +471,7 @@
         pltpu.VMEM((rows, width), BF16),
     ]
     half = layers // 2
-    sems = [(half,), (half - 1,), (2, half + 1), (2, 2, half + 1), (layers - 1, 2, SUB), (layers - 1, 2, SUB), (SUB, 2), (3,), (2,)]
+    sems = [(half - 1,), (half - 1,), (2,), (2, half + 1), (2, 2, half + 1), (layers - 1, 2, SUB), (layers - 1, 2, SUB), (SUB, 2), (3,), (2,)]
     sems += [(layers, 2), (layers,)]
     for shape in sems:
         scratch += [DMA(shape), DMA(shape)]
@@ -471,9 +481,9 @@
 
 
 def product_kernel(
-    counts, token_pos, grads, hid, slope, nrm, nin, hg, turned, b_out,
-    w_out_part, w_in_part, vec,
-    pw, hv, hw, sv, rv, nv, acc, shift, pgs, got, got_p, got_h,
+    counts, token_pos, grads, hid, slope, hg,
+    w_out_part, pgs, b_in,
+    pw, hv, hw, sv, left, shift, got, got_p, got_h,
 ):
     starts = image_starts(counts, token_pos)
     size = PATCH + 8
@@ -485,23 +495,22 @@
         bases.append(base)
         lows.append(low)
         windows.append(
-            pltpu.make_async_copy(grads.at[pl.ds(pl.multiple_of(base, 16), WINDOW)], pw.at[i], got_p.at[i])
+            pltpu.make_async_copy(
+                grads.at[pl.ds(pl.multiple_of(base, 16), WINDOW)], pw.at[pl.ds(i * WINDOW, WINDOW)], got_p.at[i]
+            )
         )
         sums.append(pltpu.make_async_copy(hg.at[pl.ds(pl.multiple_of(low, 8), size)], hw.at[i], got_h.at[i]))
-    others = [pltpu.make_async_copy(a, b, got.at[n]) for n, (a, b) in enumerate(((hid, hv), (slope, sv), (nin, rv), (nrm, nv)))]
-    for copy in [others[0], windows[0], others[1]] + sums + windows[1:] + others[2:]:
+    others = [pltpu.make_async_copy(a, b, got.at[n]) for n, (a, b) in enumerate(((hid, hv), (slope, sv)))]
+    for copy in [others[0]] + windows + [others[1]] + sums:
         copy.start()
     shift[PATCH:, :] = jnp.zeros((WINDOW - PATCH, shift.shape[1]), F32)
-    vec[16:32, :] = b_out[...]
-    vec[33:40, :] = jnp.zeros((7, 128), F32)
     others[0].wait()
     for i, start in enumerate(starts):
         shift[0:PATCH, :] = hv[i * PATCH : (i + 1) * PATCH, :].astype(F32)
-        left = pltpu.roll(shift[...], start - bases[i], 0).astype(BF16)
-        windows[i].wait()
-        product = contract(left, pw[i], 0, 0)
-        acc[...] = product if i == 0 else acc[...] + product
-    w_out_part[...] = acc[...].astype(BF16)
+        left[i * WINDOW : (i + 1) * WINDOW, :] = pltpu.roll(shift[...], start - bases[i], 0).astype(BF16)
+    for copy in windows:
+        copy.wait()
+    w_out_part[...] = contract(left[...], pw[...], 0, 0).astype(BF16)
     unit = sv.shape[1]
     total = jnp.zeros((1, unit), F32)
     others[1].wait()
@@ -513,51 +522,40 @@
         pg = (window * sv[r, :]).astype(BF16)
         pgs[r, :] = pg
         total = total + jnp.sum(pg.astype(F32), axis=0, keepdims=True)
-    vec[32:33, :] = total
-    others[2].wait()
-    w_in_part[...] = contract(pgs[...], rv[...], 0, 0).T.astype(BF16)
-    others[3].wait()
-    moment = contract(pgs[...], nv[...], 0, 0)
-    column = contract(pgs[...], jnp.ones((pgs.shape[0], 128), BF16), 0, 0)
-    for j in range(nv.shape[1] // 128):
-        at = slice(j * 128, (j + 1) * 128)
-        vec[j : j + 1, :] = jnp.sum(moment[:, at] * turned[:, at], axis=0, keepdims=True)
-        vec[8 + j : 9 + j, :] = jnp.sum(column * turned[:, at], axis=0, keepdims=True)
-
-
-def products(counts, token_pos, grads, hid, slope, nrm, nin, hg, turned, b_out):
+    b_in[...] = total
+
+
+def products(counts, token_pos, grads, hid, slope, hg):
     images = token_pos.shape[1] // PATCH
-    features, unit, quarter = nrm.shape[1], hg.shape[1], grads.shape[1]
+    unit, quarter = hg.shape[1], grads.shape[1]
     width = hid.shape[1]
     outs = (
         jax.ShapeDtypeStruct((width, quarter), BF16),
-        jax.ShapeDtypeStruct((features, unit), BF16),
-        jax.ShapeDtypeStruct((40, 128), F32),
+        jax.ShapeDtypeStruct(slope.shape, BF16),
+        jax.ShapeDtypeStruct((1, unit), F32),
     )
     scratch = [
-        pltpu.VMEM((images, WINDOW, quarter), BF16),
+        pltpu.VMEM((images * WINDOW, quarter), BF16),
         pltpu.VMEM(hid.shape, BF16),
         pltpu.VMEM((images, PATCH + 8, unit), F32),
         pltpu.VMEM(slope.shape, F32),
-        pltpu.VMEM(nin.shape, BF16),
-        pltpu.VMEM(nrm.shape, BF16),
-        pltpu.VMEM((width, quarter), F32),
+        pltpu.VMEM((images * WINDOW, width), BF16),
         pltpu.VMEM((WINDOW, width), F32),
-        pltpu.VMEM(slope.shape, BF16),
-        DMA((4,)),
+        DMA((2,)),
         DMA((images,)),
         DMA((images,)),
     ]
-    specs = [SMEM] * 2 + [ANY] * 6 + [VMEM] * 2, [VMEM] * 3
-    return call(product_kernel, outs, scratch, None, (counts, token_pos, grads, hid, slope, nrm, nin, hg, turned, b_out), 1 << 34, specs)
+    specs = [SMEM] * 2 + [ANY] * 4, [VMEM] * 3
+    return call(product_kernel, outs, scratch, None, (counts, token_pos, grads, hid, slope, hg), 1 << 34, specs)
 
 
 def last_kernel(
-    wo, wi, vec, w_out, w_in, gain, bias, b_out, b_in,
-    ry1, s1, rx1, rx2, s2, ry2, ri, v1, t1, v2, t2, v3,
+    wo_all, pgs_all, turned_all, b_out_part, b_in_part, nrm, nin,
+    w_out, w_in, gain, bias, b_out, b_in,
+    wo, pgs, turned, nv, rv, wi, vec, got, ry1, s1, rx1, rx2, s2, ry2, ri, v1, t1, v2, t2, v3,
     y1_s, y1_r, x1_s, x1_r, x2_s, x2_r, y2_s, y2_r, i_s, i_r, a_s, a_r, b_s, b_r, d_s, d_r,
 ):
-    layers, ny = v3.shape[0], wi.shape[0]
+    layers, ny = v1.shape[0], wo.shape[1]
     z, xl, c = lax.axis_index("seq_0"), lax.axis_index("seq_1"), lax.axis_index("fsdp")
     y, xh = lax.axis_index("img_0"), lax.axis_index("img_1")
 
@@ -575,7 +573,11 @@
     side_dev = [{"seq_1": 1 - xl}, {"seq_1": 1 - xl, "img_1": 1 - xh}]
     corner = {"seq_1": 1 - xl, "fsdp": 1 - c}
     stack = [{"seq_0": (z + k) % layers} for k in range(1, layers)]
-    greet(plane_dev + side_dev + [corner] + stack)
+    signal(plane_dev + side_dev + [corner] + stack)
+    pairs = ((pgs_all, pgs), (nrm, nv), (turned_all, turned), (wo_all, wo), (nin, rv))
+    loads = [pltpu.make_async_copy(source, target, got.at[n]) for n, (source, target) in enumerate(pairs)]
+    for copy in loads:
+        copy.start()
     ys = [{"img_0": (y + k) % ny} for k in range(1, ny)]
     started = []
 
@@ -584,11 +586,23 @@
         started.append(copy)
         return copy
 
+    vec[16:32, :] = b_out_part[...]
+    vec[32:33, :] = b_in_part[...]
+    vec[33:40, :] = jnp.zeros((7, 128), F32)
+    for copy in loads[:3]:
+        copy.wait()
+    moment = contract(pgs[...], nv[...], 0, 0)
+    column = contract(pgs[...], jnp.ones((pgs.shape[0], 128), BF16), 0, 0)
+    for j in range(nv.shape[1] // 128):
+        at = slice(j * 128, (j + 1) * 128)
+        vec[j : j + 1, :] = jnp.sum(moment[:, at] * turned[:, at], axis=0, keepdims=True)
+        vec[8 + j : 9 + j, :] = jnp.sum(column * turned[:, at], axis=0, keepdims=True)
+    loads[3].wait()
+    pl.semaphore_wait(pltpu.get_barrier_semaphore(), len(plane_dev) + 3 + len(stack))
     stage_a = []
-    for n, (dy, dx, dc) in enumerate(plane):
-        if dc == 0:
-            k = len(stage_a)
-            stage_a.append(go(remote(vec, v1.at[k], a_s.at[k], a_r.at[k], plane_dev[n])))
+    for k in range(1, layers):
+        stage_a.append(go(remote(vec, v1.at[z], a_s.at[k - 1], a_r.at[k - 1], stack[k - 1])))
+    v1[z] = vec[...]
     half = ry1.shape[4]
     left, right = pl.ds(0, half), pl.ds(half, half)
     across = [(1 - xl, xh), (1 - xl, 1 - xh), (xl, 1 - xh)]
@@ -599,21 +613,27 @@
     for k in range(ny - 1):
         source = wo.at[:, (y + k + 1) % ny, :, :, left]
         y_first.append(go(remote(source, ry1.at[k], y1_s.at[k], y1_r.at[k], ys[k])))
+    loads[4].wait()
+    wi[...] = contract(pgs[...], rv[...], 0, 0).T.astype(BF16).reshape(wi.shape)
     ins = []
     for n, (dy, dx, dc) in enumerate(plane):
         a, b, d = plane_ids[n]
         ins.append((go(remote(wi.at[a, b, d], ri.at[n], i_s.at[n], i_r.at[n], plane_dev[n])), n, dc))
-    total = vec[...]
-    for k, copy in enumerate(stage_a):
+
+    for copy in stage_a:
         copy.wait_recv()
-        total = total + v1[k]
-    t1[...] = total
-    q = xl * 2 + c
+    total = v1[0, 0:32]
+    for j in range(1, layers):
+        total = total + v1[j, 0:32]
+    t1[0:32] = total
+    for j in range(layers):
+        t1[32 + j : 33 + j] = v1[j, 32:33]
     stage_b = []
-    for k, (dx, dc) in enumerate(((0, 1), (1, 0), (1, 1))):
-        device = {"seq_1": flip(xl, dx), "fsdp": flip(c, dc)}
-        stage_b.append(go(remote(t1, v2.at[q], b_s.at[k], b_r.at[k], device)))
-    v2[q] = total
+    for n, (dy, dx, dc) in enumerate(plane):
+        if dc == 0:
+            k = len(stage_b)
+            stage_b.append(go(remote(t1, v2.at[k], b_s.at[k], b_r.at[k], plane_dev[n])))
+
     summed = wo[:, y, :, :, 0:half].astype(F32)
     for k, copy in enumerate(y_first):
         copy.wait_recv()
@@ -631,18 +651,18 @@
         y_second.append(
             go(remote(s2.at[:, (y + k + 1) % ny], ry2.at[k], y2_s.at[k], y2_r.at[k], ys[k]))
         )
-    for copy in stage_b:
+
+    total = t1[...]
+    for k, copy in enumerate(stage_b):
         copy.wait_recv()
-    t2[0:16] = v2[0, 0:16] + v2[1, 0:16] + v2[2, 0:16] + v2[3, 0:16]
-    t2[16:32] = v2[0, 16:32] + v2[2, 16:32]
-    t2[32:48] = v2[1, 16:32] + v2[3, 16:32]
-    for j in range(4):
-        t2[48 + j : 49 + j] = v2[j, 32:33]
-    t2[52:56] = jnp.zeros((4, 128), F32)
+        total = total + v2[k]
+    t2[...] = total
+    q = xl * 2 + c
     stage_d = []
-    for k in range(1, layers):
-        stage_d.append(go(remote(t2, v3.at[z], d_s.at[k - 1], d_r.at[k - 1], stack[k - 1])))
-    v3[z] = t2[...]
+    for k, (dx, dc) in enumerate(((0, 1), (1, 0), (1, 1))):
+        device = {"seq_1": flip(xl, dx), "fsdp": flip(c, dc)}
+        stage_d.append(go(remote(t2, v3.at[q], d_s.at[k], d_r.at[k], device)))
+    v3[q] = total
 
     same = wi[y, xh, c].astype(F32)
     cross = jnp.zeros_like(same)
@@ -673,22 +693,23 @@
 
     for copy in stage_d:
         copy.wait_recv()
-    total = v3[0]
-    for j in range(1, layers):
-        total = total + v3[j]
+    total = v3[0, 0:16] + v3[1, 0:16] + v3[2, 0:16] + v3[3, 0:16]
     gain[...] = total[0:8]
     bias[...] = total[8:16]
-    b_out[...] = total[16:48]
+    b_out[0:16, :] = v3[0, 16:32] + v3[2, 16:32]
+    b_out[16:32, :] = v3[1, 16:32] + v3[3, 16:32]
     for j in range(layers):
-        b_in[4 * j : 4 * j + 4, :] = v3[j, 48:52]
+        for n in range(4):
+            b_in[4 * j + n : 4 * j + n + 1, :] = v3[n, 32 + j : 33 + j]
     for copy in started:
         copy.wait_send()
 
 
-def last(wo, wi, vec, layers):
-    ny = wi.shape[0]
+def last(wo, pgs, turned, b_out, b_in, nrm, nin, layers):
+    ny = wo.shape[1]
     members = ny * 4 - 1
-    block = wi.shape[3:]
+    features, unit = nrm.shape[1], pgs.shape[1]
+    block = (features // (ny * 4), unit)
     rows, half = wo.shape[3], wo.shape[4] // 2
     outs = (
         jax.ShapeDtypeStruct((rows, 4 * half), F32),
@@ -699,6 +720,14 @@
         jax.ShapeDtypeStruct((4 * layers, 128), F32),
     )
     scratch = [
+        pltpu.VMEM(wo.shape, BF16),
+        pltpu.VMEM(pgs.shape, BF16),
+        pltpu.VMEM(turned.shape, F32),
+        pltpu.VMEM(nrm.shape, BF16),
+        pltpu.VMEM(nin.shape, BF16),
+        pltpu.VMEM((ny, 2, 2, *block), BF16),
+        pltpu.VMEM((40, 128), F32),
+        DMA((5,)),
         pltpu.VMEM((ny - 1, 2, 2, rows, half), BF16),
         pltpu.VMEM((2, 2, rows, half), BF16),
         pltpu.VMEM((3, rows, half), BF16),
@@ -706,15 +735,16 @@
         pltpu.VMEM((2, ny, rows, half), BF16),
         pltpu.VMEM((ny - 1, 2, rows, half), BF16),
         pltpu.VMEM((members, *block), BF16),
+        pltpu.VMEM((layers, 40, 128), F32),
+        pltpu.VMEM((40, 128), F32),
         pltpu.VMEM((2 * ny - 1, 40, 128), F32),
         pltpu.VMEM((40, 128), F32),
         pltpu.VMEM((4, 40, 128), F32),
-        pltpu.VMEM((56, 128), F32),
-        pltpu.VMEM((layers, 56, 128), F32),
     ]
-    for n in (ny - 1, 3, 3, ny - 1, members, 2 * ny - 1, 3, layers - 1):
+    for n in (ny - 1, 3, 3, ny - 1, members, layers - 1, 2 * ny - 1, 3):
         scratch += [DMA((n,)), DMA((n,))]
-    return call(last_kernel, outs, scratch, 1, (wo, wi, vec), 1 << 32)
+    specs = [ANY] * 3 + [VMEM] * 2 + [ANY] * 2, [VMEM] * 6
+    return call(last_kernel, outs, scratch, 1, (wo, pgs, turned, b_out, b_in, nrm, nin), 1 << 32, specs)
 
 
 def copy_kernel(*refs):
@@ -730,7 +760,7 @@
 
 def per_device(vision_feats, ln_gain, ln_bias, w_in, b_in, w_out, lm_grad, image_counts, token_pos):
     layers, ny = lax.axis_size("seq_0"), lax.axis_size("img_0")
-    pieces = main(
+    grads, hid, slope, nrm, nin, hg, turned, b_out_part = main(
         image_counts,
         token_pos,
         vision_feats[0],
@@ -742,9 +772,10 @@
         ln_bias[None],
         layers,
     )
-    w_out_part, w_in_part, vec = products(image_counts, token_pos, *pieces)
-    quarter, unit = w_out_part.shape[1], w_in_part.shape[1]
-    sums = last(w_out_part.reshape(2, ny, 2, -1, quarter), w_in_part.reshape(ny, 2, 2, -1, unit), vec, layers)
+    w_out_part, pgs, b_in_part = products(image_counts, token_pos, grads, hid, slope, hg)
+    quarter = w_out_part.shape[1]
+    w_out_part = w_out_part.reshape(2, ny, 2, -1, quarter)
+    sums = last(w_out_part, pgs, turned, b_out_part, b_in_part, nrm, nin, layers)
     w_out_grad, w_in_grad, gain, bias, b_out, b_in_grad = result_of(sums)
     return (w_in_grad, b_in_grad.reshape(-1), w_out_grad, b_out.reshape(-1), gain.reshape(-1), bias.reshape(-1))
 

time: 161 us -> 153 us (0.950)
  Pallas kernels: 160 us -> 152 us
    pallas_call x4, Pallas kernels: 160 us -> 152 us  [call(): pl.pallas_call(kernel, out_shape=tuple(outs), in_specs=ins, out_specs=tup...]
where the time goes in v4:
time: 153 us
  Pallas kernels  152 us (99%)
    pallas_call x4, Pallas kernels, call(): pl.pallas_call(kernel, out_shape=tuple(outs), in_specs=ins, out_specs=tup...  152 us

profile of v4, /device:TPU:1, one launch (start us, length us, event | category | flops | bytes accessed | tf_op | source)
XLA Modules:
  0.0 153.0 jit_solution(8421859124970552658)
XLA Ops:
  0.6 114.1 %shard_map.136 = (bf16[4096,1024]{1,0:T(8,128)(2,1)}, bf16[2304,512]{1,0:T(8,128)(2,1)}, f32[2304,128]{1,0:T(8,128)}, bf16[2304,1024]{1,0:T(8,128)(2,1)}, bf16[2...) custom-call(s32[1,2]{1,0:T(1,128)} %counts.3, s32[1,2304]{1,0:T(1,128)} %token_pos.3, ...), custom_call_target="tpu_custom_call" | custom-call | flops 17179869184 | bytes 1048576 | tf_op jit(solution)/shard_map/pallas_call | solution.py:47
  114.7 11.3 %shard_map.137 = (bf16[512,1024]{1,0:T(8,128)(2,1)}, bf16[2304,128]{1,0:T(8,128)(2,1)}, f32[1,128]{1,0:T(1,128)}) custom-call(s32[1,2]{1,0:T(1,128)} %counts.3, s32[1,2304]{1,0:T(1,128)} %token_pos.3, bf16[4096,1024]{1,0:T(8,128)(2,1)} %get-tuple-element.29.grads, bf16[2304,512]{1,0:T(8,128)(2,1)} %get-tuple-element.30.hid, ...), custom_call_target="tpu_custom_call" | custom-call | flops 17179869184 | bytes 1048576 | tf_op jit(solution)/shard_map/pallas_call | solution.py:47
  126.1 25.1 %shard_map.138 = (f32[32,2048]{1,0:T(8,128)}, f32[64,256]{1,0:T(8,128)}, f32[8,128]{1,0:T(8,128)}, f32[8,128]{1,0:T(8,128)}, f32[32,128]{1,0:T(8,128)}, /*index=5*/f32[32,128]{1,0:T(8,128)}) custom-call(bf16[2,4,2,32,1024]{4,3,2,1,0:T(8,128)(2,1)} %bitcast.19, bf16[2304,128]{1,0:T(8,128)(2,1)} %get-tuple-element.34.pgs_all, ...), custom_call_target="tpu_custom_call" | custom-call | flops 4294967296 | bytes 1048576 | tf_op jit(solution)/shard_map/pallas_call | solution.py:47
  151.2 1.7 %shard_map.139 = (f32[32,2048]{1,0:T(8,128)}, f32[64,256]{1,0:T(8,128)}, f32[8,128]{1,0:T(8,128)}, f32[8,128]{1,0:T(8,128)}, f32[32,128]{1,0:T(8,128)}, /*index=5*/f32[32,128]{1,0:T(8,128)}) custom-call(f32[32,2048]{1,0:T(8,128)} %get-tuple-element.40.refs_0_, f32[64,256]{1,0:T(8,128)} %get-tuple-element.41.refs_1_, f32[8,128]{1,0:T(8,128)} %get-tuple-element.42.refs_2_, ...), custom_call_target="tpu_custom_call" | custom-call | flops 1048576 | bytes 1048576 | tf_op jit(solution)/shard_map/pallas_call | solution.py:47

commit v5 on v4

--- a/solution.py
+++ b/solution.py
@@ -152,11 +152,15 @@
     def lanes(xq, cq):
         return pl.ds(pl.multiple_of((xq * 2 + cq) * unit, 128), unit)
 
-    def h_twin(s, xq):
-        return remote(mine.at[s, :, :, lanes(xq, peer)], r1.at[s, xq], h1_s.at[s, xq], h1_r.at[s, xq], twin)
-
-    def h_across(s):
-        return remote(give.at[s], r2.at[s], h2_s.at[s], h2_r.at[s], across)
+    def pair(xq):
+        return pl.ds(2 * xq, 2)
+
+    def h_twin(s, xq, side):
+        source = mine.at[s, pair(xq), :, lanes(side, peer)]
+        return remote(source, r1.at[s, side, pair(xq)], h1_s.at[s, xq, side], h1_r.at[s, xq, side], twin)
+
+    def h_across(s, xq):
+        return remote(give.at[s, pair(xq)], r2.at[s, pair(xq)], h2_s.at[s, xq], h2_r.at[s, xq], across)
 
     signal([up, down, across, twin])
     locals_ = [
@@ -221,32 +225,36 @@
     for j in range(lm.shape[1] // 128):
         column = held[:, j * 128 : (j + 1) * 128].astype(F32) * taken
         b_out[j : j + 1, :] = jnp.sum(column, axis=0, keepdims=True)
-    def multiply(s):
-        for xq in range(2):
-            for k in range(2):
-                r = rows(below(s) if k == 0 else above(s), xq, k)
-                mine[s, xq * 2 + k] = contract(grads[r, :], wq[...], 1, 1)
-        for xq in range(2):
-            h_twin(s, xq).start()
-
-    def add_twin(s):
-        for xq in range(2):
-            h_twin(s, xq).wait_recv()
-        give[s] = (mine[s, :, :, lanes(other, c)] + r1[s, other]).astype(BF16)
-        h_across(s).start()
-        for xq in range(2):
-            for k in range(2):
-                r = rows(below(s) if k == 0 else above(s), xq, k)
-                n = xq * 2 + k
-                hg[r, :] = mine[s, n, :, lanes(xl, c)] + r1[s, xl, n]
-
-    def add_across(s):
-        h_across(s).wait_recv()
-        for xq in range(2):
-            for k in range(2):
-                r = rows(below(s) if k == 0 else above(s), xq, k)
-                hg[r, :] = hg[r, :] + r2[s, xq * 2 + k].astype(F32)
-                put_sum(s, xq, k).start()
+    def part_of(g):
+        s, t = g // 2, g % 2
+        return s, xl * (1 - t) + other * t
+
+    def multiply(g):
+        s, xq = part_of(g)
+        for k in range(2):
+            r = rows(below(s) if k == 0 else above(s), xq, k)
+            mine[s, xq * 2 + k] = contract(grads[r, :], wq[...], 1, 1)
+        for side in range(2):
+            h_twin(s, xq, side).start()
+
+    def add_twin(g):
+        s, xq = part_of(g)
+        for side in range(2):
+            h_twin(s, xq, side).wait_recv()
+        give[s, pair(xq)] = (mine[s, pair(xq), :, lanes(other, c)] + r1[s, other, pair(xq)]).astype(BF16)
+        h_across(s, xq).start()
+        for k in range(2):
+            r = rows(below(s) if k == 0 else above(s), xq, k)
+            n = xq * 2 + k
+            hg[r, :] = mine[s, n, :, lanes(xl, c)] + r1[s, xl, n]
+
+    def add_across(g):
+        s, xq = part_of(g)
+        h_across(s, xq).wait_recv()
+        for k in range(2):
+            r = rows(below(s) if k == 0 else above(s), xq, k)
+            hg[r, :] = hg[r, :] + r2[s, xq * 2 + k].astype(F32)
+            put_sum(s, xq, k).start()
 
     def span(body, lo, hi):
         def step(s, carry):
@@ -350,7 +358,7 @@
                 put_layer(s, 1, n).start()
 
     def count(s):
-        return jnp.maximum(jnp.minimum(2 * s - 4, s), 0)
+        return jnp.maximum(jnp.minimum(4 * s - 8, 2 * s + 1), 0)
 
     def step(s, carry):
         serve_v(s)
@@ -369,7 +377,7 @@
                 w_twin(t, peer).wait_recv()
             turned[...] = wis[:, lanes(xl, c)].astype(F32).T
 
-        span(add_across, count(s - 3), count(s - 2))
+        span(add_across, count(s - 4), count(s - 3))
         span(add_twin, count(s - 2), count(s - 1))
         span(multiply, count(s - 1), count(s))
         serve_p(s, 1)
@@ -381,9 +389,14 @@
         return carry
 
     lax.fori_loop(1, layers, step, 0)
-    span(multiply, layers - 1, layers)
-    span(add_twin, layers - 2, layers)
-    span(add_across, layers - 3, layers)
+    last_g = 2 * layers
+    served = min(4 * (layers - 4) - 8, 2 * (layers - 4) + 1)
+    begun = min(4 * (layers - 2) - 8, 2 * (layers - 2) + 1)
+    span(multiply, last_g - 1, last_g)
+    span(add_twin, begun, last_g - 1)
+    span(add_across, served, last_g - 4)
+    span(add_twin, last_g - 1, last_g)
+    span(add_across, last_g - 4, last_g)
 
     for u in range(SUB):
         for k in range(2):
@@ -412,8 +425,9 @@
     lax.fori_loop(0, layers, put_done, 0)
     def sent_h(s):
         for xq in range(2):
-            h_twin(s, xq).wait_send()
-        h_across(s).wait_send()
+            for side in range(2):
+                h_twin(s, xq, side).wait_send()
+            h_across(s, xq).wait_send()
 
     span(sent_h, 0, layers)
     for upward in (True, False):
@@ -472,7 +486,7 @@
     ]
     half = layers // 2
     sems = [(half - 1,), (half - 1,), (2,), (2, half + 1), (2, 2, half + 1), (layers - 1, 2, SUB), (layers - 1, 2, SUB), (SUB, 2), (3,), (2,)]
-    sems += [(layers, 2), (layers,)]
+    sems += [(layers, 2, 2), (layers, 2)]
     for shape in sems:
         scratch += [DMA(shape), DMA(shape)]
     scratch += [DMA((7,)), DMA((layers, 2, 2)), DMA((half + 1, 2, 4)), DMA((layers, 2, 2))]
@@ -483,7 +497,7 @@
 def product_kernel(
     counts, token_pos, grads, hid, slope, hg,
     w_out_part, pgs, b_in,
-    pw, hv, hw, sv, left, shift, got, got_p, got_h,
+    pw, hv, hw, sv, left, got, got_p, got_h,
 ):
     starts = image_starts(counts, token_pos)
     size = PATCH + 8
@@ -500,20 +514,26 @@
             )
         )
         sums.append(pltpu.make_async_copy(hg.at[pl.ds(pl.multiple_of(low, 8), size)], hw.at[i], got_h.at[i]))
-    others = [pltpu.make_async_copy(a, b, got.at[n]) for n, (a, b) in enumerate(((hid, hv), (slope, sv)))]
-    for copy in [others[0]] + windows + [others[1]] + sums:
+    hidden = []
+    for i in range(len(starts)):
+        r = pl.ds(i * PATCH, PATCH)
+        hidden.append(pltpu.make_async_copy(hid.at[r], hv.at[r], got.at[i]))
+    slopes = pltpu.make_async_copy(slope, sv, got.at[len(starts)])
+    for copy in hidden + windows + [slopes] + sums:
         copy.start()
-    shift[PATCH:, :] = jnp.zeros((WINDOW - PATCH, shift.shape[1]), F32)
-    others[0].wait()
+    shape = (WINDOW, PATCH)
+    offset = lax.broadcasted_iota(jnp.int32, shape, 0) - lax.broadcasted_iota(jnp.int32, shape, 1)
     for i, start in enumerate(starts):
-        shift[0:PATCH, :] = hv[i * PATCH : (i + 1) * PATCH, :].astype(F32)
-        left[i * WINDOW : (i + 1) * WINDOW, :] = pltpu.roll(shift[...], start - bases[i], 0).astype(BF16)
+        place = jnp.where(offset == start - bases[i], 1.0, 0.0).astype(BF16)
+        hidden[i].wait()
+        moved = contract(place, hv[i * PATCH : (i + 1) * PATCH, :], 1, 0)
+        left[i * WINDOW : (i + 1) * WINDOW, :] = moved.astype(BF16)
     for copy in windows:
         copy.wait()
     w_out_part[...] = contract(left[...], pw[...], 0, 0).astype(BF16)
     unit = sv.shape[1]
     total = jnp.zeros((1, unit), F32)
-    others[1].wait()
+    slopes.wait()
     for i, start in enumerate(starts):
         r = slice(i * PATCH, (i + 1) * PATCH)
         sums[i].wait()
@@ -540,8 +560,7 @@
         pltpu.VMEM((images, PATCH + 8, unit), F32),
         pltpu.VMEM(slope.shape, F32),
         pltpu.VMEM((images * WINDOW, width), BF16),
-        pltpu.VMEM((WINDOW, width), F32),
-        DMA((2,)),
+        DMA((images + 1,)),
         DMA((images,)),
         DMA((images,)),
     ]
@@ -552,8 +571,8 @@
 def last_kernel(
     wo_all, pgs_all, turned_all, b_out_part, b_in_part, nrm, nin,
     w_out, w_in, gain, bias, b_out, b_in,
-    wo, pgs, turned, nv, rv, wi, vec, got, ry1, s1, rx1, rx2, s2, ry2, ri, v1, t1, v2, t2, v3,
-    y1_s, y1_r, x1_s, x1_r, x2_s, x2_r, y2_s, y2_r, i_s, i_r, a_s, a_r, b_s, b_r, d_s, d_r,
+    wo, pgs, turned, nv, rv, wi, vec, got, ry1, s1, rx1, rx2, s2, ry2, ri, v1, vo, t1, v2, t2, v3,
+    y1_s, y1_r, x1_s, x1_r, x2_s, x2_r, y2_s, y2_r, i_s, i_r, a_s, a_r, o_s, o_r, b_s, b_r, d_s, d_r,
 ):
     layers, ny = v1.shape[0], wo.shape[1]
     z, xl, c = lax.axis_index("seq_0"), lax.axis_index("seq_1"), lax.axis_index("fsdp")
@@ -574,7 +593,7 @@
     corner = {"seq_1": 1 - xl, "fsdp": 1 - c}
     stack = [{"seq_0": (z + k) % layers} for k in range(1, layers)]
     signal(plane_dev + side_dev + [corner] + stack)
-    pairs = ((pgs_all, pgs), (nrm, nv), (turned_all, turned), (wo_all, wo), (nin, rv))
+    pairs = ((wo_all, wo), (pgs_all, pgs), (nrm, nv), (turned_all, turned), (nin, rv))
     loads = [pltpu.make_async_copy(source, target, got.at[n]) for n, (source, target) in enumerate(pairs)]
     for copy in loads:
         copy.start()
@@ -586,23 +605,14 @@
         started.append(copy)
         return copy
 
-    vec[16:32, :] = b_out_part[...]
-    vec[32:33, :] = b_in_part[...]
-    vec[33:40, :] = jnp.zeros((7, 128), F32)
-    for copy in loads[:3]:
-        copy.wait()
-    moment = contract(pgs[...], nv[...], 0, 0)
-    column = contract(pgs[...], jnp.ones((pgs.shape[0], 128), BF16), 0, 0)
-    for j in range(nv.shape[1] // 128):
-        at = slice(j * 128, (j + 1) * 128)
-        vec[j : j + 1, :] = jnp.sum(moment[:, at] * turned[:, at], axis=0, keepdims=True)
-        vec[8 + j : 9 + j, :] = jnp.sum(column * turned[:, at], axis=0, keepdims=True)
-    loads[3].wait()
+    vec[16:17, :] = b_in_part[...]
+    vec[17:24, :] = jnp.zeros((7, 128), F32)
+    loads[0].wait()
     pl.semaphore_wait(pltpu.get_barrier_semaphore(), len(plane_dev) + 3 + len(stack))
-    stage_a = []
+    stage_o = []
     for k in range(1, layers):
-        stage_a.append(go(remote(vec, v1.at[z], a_s.at[k - 1], a_r.at[k - 1], stack[k - 1])))
-    v1[z] = vec[...]
+        stage_o.append(go(remote(b_out_part, vo.at[z], o_s.at[k - 1], o_r.at[k - 1], stack[k - 1])))
+    vo[z] = b_out_part[...]
     half = ry1.shape[4]
     left, right = pl.ds(0, half), pl.ds(half, half)
     across = [(1 - xl, xh), (1 - xl, 1 - xh), (xl, 1 - xh)]
@@ -613,6 +623,18 @@
     for k in range(ny - 1):
         source = wo.at[:, (y + k + 1) % ny, :, :, left]
         y_first.append(go(remote(source, ry1.at[k], y1_s.at[k], y1_r.at[k], ys[k])))
+    for copy in loads[1:4]:
+        copy.wait()
+    moment = contract(pgs[...], nv[...], 0, 0)
+    column = contract(pgs[...], jnp.ones((pgs.shape[0], 128), BF16), 0, 0)
+    for j in range(nv.shape[1] // 128):
+        at = slice(j * 128, (j + 1) * 128)
+        vec[j : j + 1, :] = jnp.sum(moment[:, at] * turned[:, at], axis=0, keepdims=True)
+        vec[8 + j : 9 + j, :] = jnp.sum(column * turned[:, at], axis=0, keepdims=True)
+    stage_a = []
+    for k in range(1, layers):
+        stage_a.append(go(remote(vec, v1.at[z], a_s.at[k - 1], a_r.at[k - 1], stack[k - 1])))
+    v1[z] = vec[...]
     loads[4].wait()
     wi[...] = contract(pgs[...], rv[...], 0, 0).T.astype(BF16).reshape(wi.shape)
     ins = []
@@ -622,12 +644,15 @@
 
     for copy in stage_a:
         copy.wait_recv()
-    total = v1[0, 0:32]
+    for copy in stage_o:
+        copy.wait_recv()
+    total, spread = v1[0, 0:16], vo[0]
     for j in range(1, layers):
-        total = total + v1[j, 0:32]
-    t1[0:32] = total
+        total, spread = total + v1[j, 0:16], spread + vo[j]
+    t1[0:16] = total
+    t1[16:32] = spread
     for j in range(layers):
-        t1[32 + j : 33 + j] = v1[j, 32:33]
+        t1[32 + j : 33 + j] = v1[j, 16:17]
     stage_b = []
     for n, (dy, dx, dc) in enumerate(plane):
         if dc == 0:
@@ -726,7 +751,7 @@
         pltpu.VMEM(nrm.shape, BF16),
         pltpu.VMEM(nin.shape, BF16),
         pltpu.VMEM((ny, 2, 2, *block), BF16),
-        pltpu.VMEM((40, 128), F32),
+        pltpu.VMEM((24, 128), F32),
         DMA((5,)),
         pltpu.VMEM((ny - 1, 2, 2, rows, half), BF16),
         pltpu.VMEM((2, 2, rows, half), BF16),
@@ -735,13 +760,14 @@
         pltpu.VMEM((2, ny, rows, half), BF16),
         pltpu.VMEM((ny - 1, 2, rows, half), BF16),
         pltpu.VMEM((members, *block), BF16),
-        pltpu.VMEM((layers, 40, 128), F32),
+        pltpu.VMEM((layers, 24, 128), F32),
+        pltpu.VMEM((layers, 16, 128), F32),
         pltpu.VMEM((40, 128), F32),
         pltpu.VMEM((2 * ny - 1, 40, 128), F32),
         pltpu.VMEM((40, 128), F32),
         pltpu.VMEM((4, 40, 128), F32),
     ]
-    for n in (ny - 1, 3, 3, ny - 1, members, layers - 1, 2 * ny - 1, 3):
+    for n in (ny - 1, 3, 3, ny - 1, members, layers - 1, layers - 1, 2 * ny - 1, 3):
         scratch += [DMA((n,)), DMA((n,))]
     specs = [ANY] * 3 + [VMEM] * 2 + [ANY] * 2, [VMEM] * 6
     return call(last_kernel, outs, scratch, 1, (wo, pgs, turned, b_out, b_in, nrm, nin), 1 << 32, specs)

time: 153 us -> 149 us (0.974)
  Pallas kernels: 152 us -> 148 us
    pallas_call x4, Pallas kernels: 152 us -> 148 us  [call(): pl.pallas_call(kernel, out_shape=tuple(outs), in_specs=ins, out_specs=tup...]
where the time goes in v5:
time: 149 us
  Pallas kernels  148 us (99%)
    pallas_call x4, Pallas kernels, call(): pl.pallas_call(kernel, out_shape=tuple(outs), in_specs=ins, out_specs=tup...  148 us

profile of v5, /device:TPU:1, one launch (start us, length us, event | category | flops | bytes accessed | tf_op | source)
XLA Modules:
  0.0 148.8 jit_solution(10137236178866453834)
XLA Ops:
  0.6 112.1 %shard_map.136 = (bf16[4096,1024]{1,0:T(8,128)(2,1)}, bf16[2304,512]{1,0:T(8,128)(2,1)}, f32[2304,128]{1,0:T(8,128)}, bf16[2304,1024]{1,0:T(8,128)(2,1)}, bf16[2...) custom-call(s32[1,2]{1,0:T(1,128)} %counts.3, s32[1,2304]{1,0:T(1,128)} %token_pos.3, ...), custom_call_target="tpu_custom_call" | custom-call | flops 17179869184 | bytes 1048576 | tf_op jit(solution)/shard_map/pallas_call | solution.py:47
  112.7 9.5 %shard_map.137 = (bf16[512,1024]{1,0:T(8,128)(2,1)}, bf16[2304,128]{1,0:T(8,128)(2,1)}, f32[1,128]{1,0:T(1,128)}) custom-call(s32[1,2]{1,0:T(1,128)} %counts.3, s32[1,2304]{1,0:T(1,128)} %token_pos.3, bf16[4096,1024]{1,0:T(8,128)(2,1)} %get-tuple-element.29.grads, bf16[2304,512]{1,0:T(8,128)(2,1)} %get-tuple-element.30.hid, ...), custom_call_target="tpu_custom_call" | custom-call | flops 17179869184 | bytes 1048576 | tf_op jit(solution)/shard_map/pallas_call | solution.py:47
  122.2 24.9 %shard_map.138 = (f32[32,2048]{1,0:T(8,128)}, f32[64,256]{1,0:T(8,128)}, f32[8,128]{1,0:T(8,128)}, f32[8,128]{1,0:T(8,128)}, f32[32,128]{1,0:T(8,128)}, /*index=5*/f32[32,128]{1,0:T(8,128)}) custom-call(bf16[2,4,2,32,1024]{4,3,2,1,0:T(8,128)(2,1)} %bitcast.19, bf16[2304,128]{1,0:T(8,128)(2,1)} %get-tuple-element.34.pgs_all, ...), custom_call_target="tpu_custom_call" | custom-call | flops 4294967296 | bytes 1048576 | tf_op jit(solution)/shard_map/pallas_call | solution.py:47
  147.1 1.7 %shard_map.139 = (f32[32,2048]{1,0:T(8,128)}, f32[64,256]{1,0:T(8,128)}, f32[8,128]{1,0:T(8,128)}, f32[8,128]{1,0:T(8,128)}, f32[32,128]{1,0:T(8,128)}, /*index=5*/f32[32,128]{1,0:T(8,128)}) custom-call(f32[32,2048]{1,0:T(8,128)} %get-tuple-element.40.refs_0_, f32[64,256]{1,0:T(8,128)} %get-tuple-element.41.refs_1_, f32[8,128]{1,0:T(8,128)} %get-tuple-element.42.refs_2_, ...), custom_call_target="tpu_custom_call" | custom-call | flops 1048576 | bytes 1048576 | tf_op jit(solution)/shard_map/pallas_call | solution.py:47

commit v6 on v5

--- a/solution.py
+++ b/solution.py
@@ -340,22 +340,17 @@
         for upward in (True, False):
             put_chunk(s, t, upward).start()
 
-    def use_v(s):
-        @pl.when(s <= v_up)
+    def use_v(s, d):
+        layer = below(s) if d == 0 else above(s)
+        wanted = s <= v_up if d == 0 else (s >= 1) & (s <= v_down)
+
+        @pl.when(wanted)
         def _():
-            v_twin(s, 0, xl, 0, peer).wait_recv()
-            v_twin(s, 0, other, 1, peer).wait_recv()
-            normalise(below(s))
+            v_twin(s, d, xl, 0, peer).wait_recv()
+            v_twin(s, d, other, 1, peer).wait_recv()
+            normalise(layer)
             for n in range(4):
-                put_layer(s, 0, n).start()
-
-        @pl.when((s >= 1) & (s <= v_down))
-        def _():
-            v_twin(s, 1, xl, 0, peer).wait_recv()
-            v_twin(s, 1, other, 1, peer).wait_recv()
-            normalise(above(s))
-            for n in range(4):
-                put_layer(s, 1, n).start()
+                put_layer(s, d, n).start()
 
     def count(s):
         return jnp.maximum(jnp.minimum(4 * s - 8, 2 * s + 1), 0)
@@ -380,11 +375,16 @@
         span(add_across, count(s - 4), count(s - 3))
         span(add_twin, count(s - 2), count(s - 1))
         span(multiply, count(s - 1), count(s))
-        serve_p(s, 1)
 
         @pl.when(s >= 3)
         def _():
-            use_v(s - 3)
+            use_v(s - 3, 0)
+
+        serve_p(s, 1)
+
+        @pl.when(s >= 3)
+        def _():
+            use_v(s - 3, 1)
 
         return carry
 
@@ -497,7 +497,7 @@
 def product_kernel(
     counts, token_pos, grads, hid, slope, hg,
     w_out_part, pgs, b_in,
-    pw, hv, hw, sv, left, got, got_p, got_h,
+    pw, hv, hw, sv, left, result, got, got_p, got_h,
 ):
     starts = image_starts(counts, token_pos)
     size = PATCH + 8
@@ -530,7 +530,9 @@
         left[i * WINDOW : (i + 1) * WINDOW, :] = moved.astype(BF16)
     for copy in windows:
         copy.wait()
-    w_out_part[...] = contract(left[...], pw[...], 0, 0).astype(BF16)
+    result[...] = contract(left[...], pw[...], 0, 0).astype(BF16)
+    put = pltpu.make_async_copy(result, w_out_part, got.at[len(starts) + 1])
+    put.start()
     unit = sv.shape[1]
     total = jnp.zeros((1, unit), F32)
     slopes.wait()
@@ -543,6 +545,7 @@
         pgs[r, :] = pg
         total = total + jnp.sum(pg.astype(F32), axis=0, keepdims=True)
     b_in[...] = total
+    put.wait()
 
 
 def products(counts, token_pos, grads, hid, slope, hg):
@@ -560,11 +563,12 @@
         pltpu.VMEM((images, PATCH + 8, unit), F32),
         pltpu.VMEM(slope.shape, F32),
         pltpu.VMEM((images * WINDOW, width), BF16),
-        DMA((images + 1,)),
+        pltpu.VMEM((width, quarter), BF16),
+        DMA((images + 2,)),
         DMA((images,)),
         DMA((images,)),
     ]
-    specs = [SMEM] * 2 + [ANY] * 4, [VMEM] * 3
+    specs = [SMEM] * 2 + [ANY] * 4, [ANY] + [VMEM] * 2
     return call(product_kernel, outs, scratch, None, (counts, token_pos, grads, hid, slope, hg), 1 << 34, specs)
 
 

time: 149 us -> 148 us (level)
  no operation moved by 1% of the time
where the time goes in v6:
time: 148 us
  Pallas kernels  147 us (99%)
    pallas_call x4, Pallas kernels, call(): pl.pallas_call(kernel, out_shape=tuple(outs), in_specs=ins, out_specs=tup...  147 us

profile of v6, /device:TPU:1, one launch (start us, length us, event | category | flops | bytes accessed | tf_op | source)
XLA Modules:
  0.0 147.9 jit_solution(9505364805425776813)
XLA Ops:
  0.6 111.2 %shard_map.136 = (bf16[4096,1024]{1,0:T(8,128)(2,1)}, bf16[2304,512]{1,0:T(8,128)(2,1)}, f32[2304,128]{1,0:T(8,128)}, bf16[2304,1024]{1,0:T(8,128)(2,1)}, bf16[2...) custom-call(s32[1,2]{1,0:T(1,128)} %counts.3, s32[1,2304]{1,0:T(1,128)} %token_pos.3, ...), custom_call_target="tpu_custom_call" | custom-call | flops 17179869184 | bytes 1048576 | tf_op jit(solution)/shard_map/pallas_call | solution.py:47
  111.8 9.5 %shard_map.137 = (bf16[512,1024]{1,0:T(8,128)(2,1)}, bf16[2304,128]{1,0:T(8,128)(2,1)}, f32[1,128]{1,0:T(1,128)}) custom-call(s32[1,2]{1,0:T(1,128)} %counts.3, s32[1,2304]{1,0:T(1,128)} %token_pos.3, bf16[4096,1024]{1,0:T(8,128)(2,1)} %get-tuple-element.29.grads, bf16[2304,512]{1,0:T(8,128)(2,1)} %get-tuple-element.30.hid, ...), custom_call_target="tpu_custom_call" | custom-call | flops 17179869184 | bytes 1048576 | tf_op jit(solution)/shard_map/pallas_call | solution.py:47
  121.3 24.9 %shard_map.138 = (f32[32,2048]{1,0:T(8,128)}, f32[64,256]{1,0:T(8,128)}, f32[8,128]{1,0:T(8,128)}, f32[8,128]{1,0:T(8,128)}, f32[32,128]{1,0:T(8,128)}, /*index=5*/f32[32,128]{1,0:T(8,128)}) custom-call(bf16[2,4,2,32,1024]{4,3,2,1,0:T(8,128)(2,1)} %bitcast.19, bf16[2304,128]{1,0:T(8,128)(2,1)} %get-tuple-element.34.pgs_all, ...), custom_call_target="tpu_custom_call" | custom-call | flops 4294967296 | bytes 1048576 | tf_op jit(solution)/shard_map/pallas_call | solution.py:47
  146.2 1.7 %shard_map.139 = (f32[32,2048]{1,0:T(8,128)}, f32[64,256]{1,0:T(8,128)}, f32[8,128]{1,0:T(8,128)}, f32[8,128]{1,0:T(8,128)}, f32[32,128]{1,0:T(8,128)}, /*index=5*/f32[32,128]{1,0:T(8,128)}) custom-call(f32[32,2048]{1,0:T(8,128)} %get-tuple-element.40.refs_0_, f32[64,256]{1,0:T(8,128)} %get-tuple-element.41.refs_1_, f32[8,128]{1,0:T(8,128)} %get-tuple-element.42.refs_2_, ...), custom_call_target="tpu_custom_call" | custom-call | flops 1048576 | bytes 1048576 | tf_op jit(solution)/shard_map/pallas_call | solution.py:47
